TPU v7x, 32 devices: a whole 2x2x4 slice. The times are simulated.
32 devices in a mesh: seq: 8 (over y, x, core), batch: 4 (over z).
Axes of the slice: x: 2, y: 2, z: 4, core: 2. Of those that a mesh axis runs over, the one named last changes fastest.
Arguments:
- queries: bfloat16 [4096, 4096], P(('batch', 'seq')), parts along dimension 0, may hold values from -6 to 6
- key_vectors: bfloat16 [4096, 4096], P(('batch', 'seq')), parts along dimension 0, may hold values from -6 to 6
- value_vectors: bfloat16 [4096, 4096], P(('batch', 'seq')), parts along dimension 0, may hold values from -6 to 6
- residual_in: bfloat16 [4096, 4096], P(('batch', 'seq')), parts along dimension 0, may hold values from -6 to 6
- input_logit: float32 [8, 4096], P(None, ('batch', 'seq')), parts along dimension 1, may hold values from -8 to 300
- forget_logit: float32 [8, 4096], P(None, ('batch', 'seq')), parts along dimension 1, may hold values from -3 to 13
- mix_gain: float32 [4096], replicated, may hold values from 0.1 to 1.9
- ffn_gain: float32 [4096], replicated, may hold values from 0.1 to 1.9
- expert_gate: bfloat16 [8, 4096, 704], P('seq'), may hold values from -0.09375 to 0.09375
- expert_up: bfloat16 [8, 4096, 704], P('seq'), may hold values from -0.09375 to 0.09375
- expert_down: bfloat16 [8, 704, 4096], P('seq'), may hold values from -0.21875 to 0.21875
- routes: int32 [4096, 2], P(('batch', 'seq')), parts along dimension 0, may hold values from 0 to 7, all different within a row; in each aligned block of 128 rows (0 to 127, 128 to 255, ...) at most 64 rows name the same one
- route_weight: float32 [4096, 2], P(('batch', 'seq')), parts along dimension 0, may hold values from 0.2 to 1
Outputs:
- block_out: bfloat16 [4096, 4096], P(('batch', 'seq')), parts along dimension 0
There are 4 independent parts, one for each index of `batch`. A program takes and returns all parts, laid end to end along the dimension named above; an argument that names none is the same for every part. Nothing has to cross between parts.
Inputs may be any that keep to these rules, and one draw needn't show every extreme that they name: `routes`: each row names two different experts. Within the rows of one device no expert is named by more than 64 rows, and in some device one expert is named by exactly 64 rows.
All inputs are finite; a program needn't handle non-finite values.
Results may differ from a plain program's by a relative error of at most 0.0081.
Values may be sent and summed in bfloat16 or wider, within the bound.
A program may use at most 128 MiB of HBM per device.

v0:
```python
import functools
import math

import jax
import jax.numpy as jnp
from jax import lax
from jax.experimental import pallas as pl
from jax.experimental.pallas import tpu as pltpu
from jax.sharding import PartitionSpec as P

EPSILON = 1e-06
PIECES = 4


def exchange_kernel(moves, devices, *refs):
    count = len(moves)
    sources, targets = refs[:count], refs[count : 2 * count]
    send_sem, recv_sem, local_sem = refs[2 * count :]
    me = lax.axis_index("seq")
    others = [lax.rem(me + step, devices) for step in range(1, devices)]
    barrier = pltpu.get_barrier_semaphore()
    for other in others:
        pl.semaphore_signal(
            barrier, inc=1, device_id={"seq": other}, device_id_type=pl.DeviceIdType.MESH
        )
    pl.semaphore_wait(barrier, devices - 1)
    copies = []
    for i, (take, put) in enumerate(moves):
        for step, other in enumerate(others):
            copies.append(
                pltpu.make_async_remote_copy(
                    src_ref=take(sources[i], other),
                    dst_ref=put(targets[i], me),
                    send_sem=send_sem.at[i, step],
                    recv_sem=recv_sem.at[i, step],
                    device_id={"seq": other},
                    device_id_type=pl.DeviceIdType.MESH,
                )
            )
            copies[-1].start()
    for i, (take, put) in enumerate(moves):
        copies.append(
            pltpu.make_async_copy(take(sources[i], me), put(targets[i], me), local_sem.at[i])
        )
        copies[-1].start()
    for copy in copies:
        copy.wait()


def exchange(moves, devices, number, sources, shapes):
    far = pl.BlockSpec(memory_space=pl.ANY)
    count = len(moves)
    return pl.pallas_call(
        functools.partial(exchange_kernel, moves, devices),
        out_shape=shapes,
        in_specs=[far] * count,
        out_specs=[far] * count,
        scratch_shapes=[
            pltpu.SemaphoreType.DMA((count, devices - 1)),
            pltpu.SemaphoreType.DMA((count, devices - 1)),
            pltpu.SemaphoreType.DMA((count,)),
        ],
        compiler_params=pltpu.CompilerParams(collective_id=number, has_side_effects=True),
    )(*sources)


def head_mix(query, key, value, input_gate, forget_gate):
    positions, head_dim = query.shape
    cumul_log = jnp.cumsum(jax.nn.log_sigmoid(forget_gate))
    level = input_gate - cumul_log
    top = lax.cummax(level, axis=0)
    scores = lax.dot_general(
        query, key, (((1,), (1,)), ((), ())), preferred_element_type=jnp.float32
    )
    causal = jnp.arange(positions)[:, None] >= jnp.arange(positions)[None, :]
    decay = jnp.exp(jnp.minimum(level[None, :] - top[:, None], 0.0))
    coef = jnp.where(causal, decay * scores, 0.0) * (1.0 / math.sqrt(head_dim))
    denom_sum = jnp.sum(coef, axis=1, keepdims=True)
    numer_sum = jnp.dot(coef.astype(jnp.bfloat16), value, preferred_element_type=jnp.float32)
    return numer_sum / jnp.maximum(jnp.abs(denom_sum), 1.0)


def expert_kernel(
    normed,
    updated,
    pick,
    pick_back,
    slot_weight,
    gate_far,
    up_far,
    down_far,
    out,
    blocks,
    gate,
    up,
    down,
    rows,
    gate_sum,
    up_sum,
    hidden,
    core_out,
    own,
    core_in,
    hop_out,
    hop_in,
    keep,
    last_out,
    last_in,
    load_sem,
    gather_send,
    gather_recv,
    core_send,
    core_recv,
    hop_send,
    hop_recv,
    last_send,
    last_recv,
):
    me = lax.axis_index("seq")
    width = rows.shape[1]
    capacity = pick.shape[1]

    def peer(flip):
        total = 0
        for bit in (1, 2, 4):
            own_bit = lax.rem(lax.div(me, bit), 2)
            total = total + bit * ((1 - own_bit) if flip & bit else own_bit)
        return {"seq": total}

    def remote(source, target, send_sem, recv_sem, flip):
        return pltpu.make_async_remote_copy(
            src_ref=source,
            dst_ref=target,
            send_sem=send_sem,
            recv_sem=recv_sem,
            device_id=peer(flip),
            device_id_type=pl.DeviceIdType.MESH,
        )

    loads = [
        pltpu.make_async_copy(far, near, load_sem.at[i])
        for i, (far, near) in enumerate(((gate_far, gate), (up_far, up), (down_far, down)))
    ]
    for load in loads:
        load.start()
    barrier = pltpu.get_barrier_semaphore()
    for flip in (1, 2, 4):
        pl.semaphore_signal(
            barrier, inc=1, device_id=peer(flip), device_id_type=pl.DeviceIdType.MESH
        )
    pl.semaphore_wait(barrier, 3)

    def columns(piece):
        return pl.ds(piece * width, width)

    def block(slot, piece):
        return normed.at[:, columns(piece)] if slot == 0 else blocks.at[slot - 1, piece]

    gathers = {}
    for piece in range(PIECES):
        across = (4, 2) if piece % 2 == 0 else (2, 4)
        for slot, source, flip in (
            (1, 0, 1),
            (2, 0, 2),
            (4, 0, 4),
            (6,) + across,
            (3, 2, 1),
            (5, 4, 1),
            (7, 6, 1),
        ):
            gathers[slot, piece] = remote(
                block(source, piece),
                block(slot, piece),
                gather_send.at[slot - 1, piece],
                gather_recv.at[slot - 1, piece],
                flip,
            )

    def send_own(piece):
        for slot in (2, 4, 1):
            gathers[slot, piece].start()

    def first_products(piece):
        for slot in (1, 3, 5, 7):
            gathers[slot, piece].wait_recv()
        if piece == 0:
            loads[0].wait()
            loads[1].wait()
        for slot in range(8):
            rows[slot * capacity : (slot + 1) * capacity, :] = jnp.dot(
                pick[slot], block(slot, piece)[...], preferred_element_type=jnp.float32
            ).astype(jnp.bfloat16)
        for weight, total in ((gate, gate_sum), (up, up_sum)):
            term = lax.dot_general(
                rows[...],
                weight[:, columns(piece)],
                (((1,), (1,)), ((), ())),
                preferred_element_type=jnp.float32,
            )
            total[...] = term if piece == 0 else total[...] + term

    send_own(0)
    send_own(1)
    for piece in range(PIECES):
        gathers[2, piece].wait_recv()
        gathers[4, piece].wait_recv()
        for slot in (6, 3, 5):
            gathers[slot, piece].start()
        if piece + 2 < PIECES:
            send_own(piece + 2)
        gathers[6, piece].wait_recv()
        gathers[7, piece].start()
        if piece > 0:
            first_products(piece - 1)
    first_products(PIECES - 1)
    gate_val = gate_sum[...]
    hidden[...] = (gate_val / (1.0 + jnp.exp(-gate_val)) * up_sum[...]).astype(jnp.bfloat16)
    loads[2].wait()

    core_copies, hop_copies, last_copies = {}, {}, {}

    def second_product(piece):
        rows[...] = (
            jnp.dot(hidden[...], down[:, columns(piece)], preferred_element_type=jnp.float32)
            * slot_weight[...]
        ).astype(jnp.bfloat16)
        for slot in (7, 5, 3, 1, 6, 4, 2, 0):
            part = jnp.dot(
                pick_back[slot],
                rows[slot * capacity : (slot + 1) * capacity, :],
                preferred_element_type=jnp.float32,
            ).astype(jnp.bfloat16)
            half = slot // 2
            if slot % 2 == 0:
                own[half, piece] = part
                continue
            core_out[half, piece] = part
            core_copies[half, piece] = remote(
                core_out.at[half, piece],
                core_in.at[half, piece],
                core_send.at[half, piece],
                core_recv.at[half, piece],
                1,
            )
            core_copies[half, piece].start()

    def first_hop(piece):
        first, second = (2, 4) if piece % 2 == 0 else (4, 2)
        for slot in (6, first, second, 0):
            half = slot // 2
            core_copies[half, piece].wait_recv()
            both = own[half, piece].astype(jnp.float32) + core_in[half, piece].astype(jnp.float32)
            if slot in (0, second):
                keep[0 if slot == 0 else 1, piece] = both
                continue
            place = 1 if slot == 6 else 0
            hop_out[place, piece] = both.astype(jnp.bfloat16)
            hop_copies[place, piece] = remote(
                hop_out.at[place, piece],
                hop_in.at[place, piece],
                hop_send.at[place, piece],
                hop_recv.at[place, piece],
                first,
            )
            hop_copies[place, piece].start()

    def second_hop(piece):
        second = 4 if piece % 2 == 0 else 2
        hop_copies[1, piece].wait_recv()
        last_out[piece] = (keep[1, piece] + hop_in[1, piece].astype(jnp.float32)).astype(
            jnp.bfloat16
        )
        last_copies[piece] = remote(
            last_out.at[piece], last_in.at[piece], last_send.at[piece], last_recv.at[piece], second
        )
        last_copies[piece].start()

    def finish(piece):
        hop_copies[0, piece].wait_recv()
        last_copies[piece].wait_recv()
        out[:, columns(piece)] = (
            updated[:, columns(piece)].astype(jnp.float32)
            + (
                keep[0, piece]
                + hop_in[0, piece].astype(jnp.float32)
                + last_in[piece].astype(jnp.float32)
            )
        ).astype(jnp.bfloat16)

    for piece in range(PIECES):
        second_product(piece)
        if piece > 0:
            first_hop(piece - 1)
    first_hop(PIECES - 1)
    for piece in range(PIECES):
        second_hop(piece)
        if piece > 0:
            finish(piece - 1)
    finish(PIECES - 1)
    for copies in (gathers, core_copies, hop_copies, last_copies):
        for copy in copies.values():
            copy.wait_send()


def cube_experts(normed, updated, pick, slot_weight, gate_weight, up_weight, down_weight):
    tokens, model_width = normed.shape
    hidden_width = gate_weight.shape[0]
    slots = slot_weight.shape[0]
    width = model_width // PIECES
    near = pl.BlockSpec(memory_space=pltpu.VMEM)
    far = pl.BlockSpec(memory_space=pl.ANY)

    def pieces(*lead, kind=jnp.bfloat16):
        return pltpu.VMEM(lead + (PIECES, tokens, width), kind)

    def flags(*shape):
        return pltpu.SemaphoreType.DMA(shape)

    return pl.pallas_call(
        expert_kernel,
        out_shape=jax.ShapeDtypeStruct((tokens, model_width), jnp.bfloat16),
        in_specs=[near] * 5 + [far] * 3,
        out_specs=near,
        scratch_shapes=[
            pieces(7),
            pltpu.VMEM(gate_weight.shape, jnp.bfloat16),
            pltpu.VMEM(up_weight.shape, jnp.bfloat16),
            pltpu.VMEM(down_weight.shape, jnp.bfloat16),
            pltpu.VMEM((slots, width), jnp.bfloat16),
            pltpu.VMEM((slots, hidden_width), jnp.float32),
            pltpu.VMEM((slots, hidden_width), jnp.float32),
            pltpu.VMEM((slots, hidden_width), jnp.bfloat16),
            pieces(4),
            pieces(4),
            pieces(4),
            pieces(2),
            pieces(2),
            pieces(2, kind=jnp.float32),
            pieces(),
            pieces(),
            flags(3),
            flags(7, PIECES),
            flags(7, PIECES),
            flags(4, PIECES),
            flags(4, PIECES),
            flags(2, PIECES),
            flags(2, PIECES),
            flags(PIECES),
            flags(PIECES),
        ],
        compiler_params=pltpu.CompilerParams(
            collective_id=1, has_side_effects=True, vmem_limit_bytes=67043328
        ),
    )(
        normed,
        updated,
        pick,
        jnp.transpose(pick, (0, 2, 1)),
        slot_weight,
        gate_weight,
        up_weight,
        down_weight,
    )


def shards(
    queries,
    key_vectors,
    value_vectors,
    residual_in,
    input_logit,
    forget_logit,
    mix_gain,
    ffn_gain,
    expert_gate,
    expert_up,
    expert_down,
    routes,
    route_weight,
):
    tokens, model_width = queries.shape
    head_count = input_logit.shape[0]
    head_dim = model_width // head_count
    devices = lax.axis_size("seq")
    group = devices // head_count
    group_width = model_width // devices

    capacity = 4 * tokens // devices
    flat_routes = routes.reshape(-1)
    matches = (flat_routes[:, None] == jnp.arange(devices, dtype=jnp.int32)[None, :]).astype(
        jnp.int32
    )
    before = jnp.cumsum(matches, axis=0) - matches
    position = jnp.sum(before * matches, axis=1)
    position = position.reshape(tokens, 2)
    slot_index = (flat_routes * capacity + position.reshape(-1)).reshape(tokens, 2)
    notes = jnp.stack(
        (jnp.repeat(input_logit, group, axis=0), jnp.repeat(forget_logit, group, axis=0)), axis=1
    )
    routing = jnp.concatenate(
        (routes.astype(jnp.float32), position.astype(jnp.float32), route_weight), axis=1
    )
    routing = jnp.broadcast_to(jnp.transpose(routing)[None], (devices, 6, tokens))
    notes = jnp.concatenate((notes, routing), axis=1)

    def columns_of(width, share):
        return lambda ref, other: ref.at[
            :, pl.ds(pl.multiple_of((other // share) * width, width), width)
        ]

    def rows_from(ref, origin):
        return ref.at[pl.ds(pl.multiple_of(origin * tokens, tokens), tokens), :]

    def entry(ref, other):
        return ref.at[other]

    head_columns = columns_of(head_dim, group)
    own_columns = columns_of(group_width, 1)
    tall = devices * tokens
    told, key_all, query_all, value_all = exchange(
        (
            (entry, entry),
            (head_columns, rows_from),
            (head_columns, rows_from),
            (own_columns, rows_from),
        ),
        devices,
        2,
        (notes, key_vectors, queries, value_vectors),
        (
            jax.ShapeDtypeStruct(notes.shape, jnp.float32),
            jax.ShapeDtypeStruct((tall, head_dim), jnp.bfloat16),
            jax.ShapeDtypeStruct((tall, head_dim), jnp.bfloat16),
            jax.ShapeDtypeStruct((tall, group_width), jnp.bfloat16),
        ),
    )
    mixed = head_mix(
        query_all, key_all, value_all, told[:, 0].reshape(-1), told[:, 1].reshape(-1)
    ).astype(jnp.bfloat16)
    (mixer_out,) = exchange(
        ((rows_from, own_columns),),
        devices,
        3,
        (mixed,),
        (jax.ShapeDtypeStruct((tokens, model_width), jnp.bfloat16),),
    )
    mixer_out = mixer_out.astype(jnp.float32)
    mixer_square = jnp.mean(mixer_out * mixer_out, axis=1, keepdims=True)
    updated = (
        residual_in.astype(jnp.float32) + mixer_out * lax.rsqrt(mixer_square + EPSILON) * mix_gain
    ).astype(jnp.bfloat16)
    updated_float = updated.astype(jnp.float32)
    updated_square = jnp.mean(updated_float * updated_float, axis=1, keepdims=True)
    normed = (updated_float * lax.rsqrt(updated_square + EPSILON) * ffn_gain).astype(jnp.bfloat16)
    if devices == 8:
        me = lax.axis_index("seq")
        told = told[jnp.bitwise_xor(me, jnp.arange(devices, dtype=jnp.int32))]
        mine = me.astype(jnp.float32)
        places = jnp.where(told[:, 2:4] == mine, told[:, 4:6], -1.0)
        slots = jnp.arange(capacity, dtype=jnp.float32)[None, :, None]
        pick_one = places[:, 0:1] == slots
        pick_two = places[:, 1:2] == slots
        slot_weight = jnp.sum(
            jnp.where(pick_one, told[:, 6:7], 0.0) + jnp.where(pick_two, told[:, 7:8], 0.0),
            axis=2,
        ).reshape(devices * capacity, 1)
        pick = jnp.logical_or(pick_one, pick_two).astype(jnp.bfloat16)
        return cube_experts(
            normed,
            updated,
            pick,
            slot_weight,
            jnp.transpose(expert_gate[0]),
            jnp.transpose(expert_up[0]),
            expert_down[0],
        )
    columns = jnp.arange(devices * capacity, dtype=jnp.int32)
    pick_first = (slot_index[:, 0:1] == columns[None, :]).astype(jnp.bfloat16)
    pick_second = (slot_index[:, 1:2] == columns[None, :]).astype(jnp.bfloat16)
    spread = jnp.einsum(
        "tc,td->cd", pick_first + pick_second, normed, preferred_element_type=jnp.float32
    ).astype(jnp.bfloat16)
    outbound = spread.reshape(devices, capacity, model_width)
    block_in = lax.all_to_all(outbound, "seq", split_axis=0, concat_axis=0, tiled=True)
    row_block = block_in.reshape(-1, model_width)
    gate_val = jnp.dot(row_block, expert_gate[0], preferred_element_type=jnp.float32)
    up_val = jnp.dot(row_block, expert_up[0], preferred_element_type=jnp.float32)
    hidden = (jax.nn.silu(gate_val) * up_val).astype(jnp.bfloat16)
    result = jnp.dot(hidden, expert_down[0], preferred_element_type=jnp.float32).astype(
        jnp.bfloat16
    )
    inbound = lax.all_to_all(
        result.reshape(block_in.shape), "seq", split_axis=0, concat_axis=0, tiled=True
    )
    flat_back = inbound.reshape(devices * capacity, model_width)
    first_out = jnp.dot(pick_first, flat_back, preferred_element_type=jnp.float32)
    second_out = jnp.dot(pick_second, flat_back, preferred_element_type=jnp.float32)
    expert_mix = route_weight[:, 0:1] * first_out + route_weight[:, 1:2] * second_out
    return (updated_float + expert_mix).astype(jnp.bfloat16)


def solution(mesh):
    return jax.shard_map(
        shards,
        mesh=mesh,
        in_specs=(
            P(("batch", "seq"), None),
            P(("batch", "seq"), None),
            P(("batch", "seq"), None),
            P(("batch", "seq"), None),
            P(None, ("batch", "seq")),
            P(None, ("batch", "seq")),
            P(),
            P(),
            P("seq", None, None),
            P("seq", None, None),
            P("seq", None, None),
            P(("batch", "seq"), None),
            P(("batch", "seq"), None),
        ),
        out_specs=P(("batch", "seq"), None),
        check_vma=False,
    )
```

profile of v0, /device:TPU:0, one launch (start us, length us, event | category | flops | bytes accessed | tf_op | source)
XLA Modules:
  0.0 177.4 jit_solution(14110054549959572356)
XLA Ops:
  0.0 0.8 copy.20
  0.8 0.1 eq.79
  0.9 0.6 reduce-window.24
  1.5 0.2 slice_reduce_fusion
  1.8 0.1 eq.75
  1.9 0.1 fusion.18
  2.0 0.1 convert_element_type.50
  2.2 0.7 convert_element_type.46
  2.9 0.7 maximum_bitcast_fusion
  3.6 1.3 pad_maximum_fusion.refs_0_
  5.0 39.4 %shard_map.127 = (f32[8,8,128]{2,1,0:T(8,128)}, bf16[1024,512]{1,0:T(8,128)(2,1)}, bf16[1024,512]{1,0:T(8,128)(2,1)}, bf16[1024,512]{1,0:T(8,128)(2,1)}) custom-call(f32[8,8,128]{2,1,0:T(8,128)} %pad_maximum_fusion.refs_0_, bf16[128,4096]{1,0:T(8,128)(2,1)} %refs_1_.1, bf16[128,4096]{1,0:T(8,128)(2,1)} %refs_2_.1, bf16[128,4096]{1,0:T(8,128)(2,1)} %refs_3_.1), custom_call_target="tpu_custom_call" | custom-call | tf_op jit(solution)/shard_map/pallas_call | solution.py:53
  44.4 0.8 slice_negate_fusion
  45.3 0.3 reduce-window.26
  45.6 0.1 slice.48
  45.7 0.1 slice_reduce_fusion.2
  45.8 0.1 add_subtract_fusion
  45.9 0.3 reduce-window.36
  46.3 0.1 slice_reduce_fusion.1
  46.5 3.0 %fusion = (f32[1024]{0:T(1024)S(1)}, f32[1024,1024]{0,1:T(8,128)S(1)}) fusion(f32[1024]{0:T(1024)S(1)} %maximum_bitcast_fusion.1, f32[1024]{0:T(1024)S(1)} %bitcast_subtract_fusion.1, bf16[1024,512]{1,0:T(8,128)(2,1)} %get-tuple-element.10, bf16[1024,512]{1,0:T(8,128)(2,1)} %get-tuple-element.11), kind=kOutput, calls=%fused_computation.7 | convolution fusion | flops 1081080832 | bytes 6303744 | tf_op jit(solution)/shard_map/dot_general | solution.py:72
  49.6 2.4 %divide_convert_fusion.refs_0_ = bf16[1024,512]{1,0:T(8,128)(2,1)} fusion(f32[1024]{0:T(1024)S(1)} %abs_maximum_fusion, bf16[1024,512]{1,0:T(8,128)(2,1)S(1)} %copy-done.5, f32[1024,1024]{0,1:T(8,128)S(1)} %get-tuple-element.22, f32[1024]{0:T(1024)S(1)} %maximum_bitcast_fusion.1, f32[1024]{0:T(1024)S(1)} %bitcast_subtract_fusion.1), kind=kOutput, calls=%fused_computation.16 | convolution fusion | flops 1082130432 | bytes 6303744 | tf_op jit(solution)/shard_map/dot_general | solution.py:79
  52.0 15.0 %shard_map.128 = bf16[128,4096]{1,0:T(8,128)(2,1)} custom-call(bf16[1024,512]{1,0:T(8,128)(2,1)} %divide_convert_fusion.refs_0_), custom_call_target="tpu_custom_call" | custom-call | tf_op jit(solution)/shard_map/pallas_call | solution.py:53
  67.0 1.5 fusion.2
  68.5 2.0 %fusion.6 = (f32[128]{0:T(128)S(1)}, bf16[128,4096]{1,0:T(8,128)(2,1)S(1)}) fusion(f32[4096]{0:T(1024)S(1)} %copy-done.3, f32[128]{0:T(128)S(1)} %add_rsqrt_fusion.1, bf16[128,4096]{1,0:T(8,128)(2,1)} %shard_map.128, bf16[128,4096]{1,0:T(8,128)(2,1)S(1)} %copy-done.1), kind=kLoop, calls=%fused_computation.13 | loop fusion | flops 4718464 | bytes 3163136 | tf_op jit(solution)/shard_map/reduce_sum | solution.py:453
  70.5 1.0 copy-done
  71.5 1.3 fusion.8.normed
  72.8 0.6 gather_fusion
  73.4 0.1 add_reduce_fusion
  73.6 0.9 reshape.127.slot_weight
  74.5 1.1 fusion.14.pick_back
  75.6 0.7 fusion.16.pick
  76.2 98.9 %shard_map.129 = bf16[128,4096]{1,0:T(8,128)(2,1)} custom-call(bf16[128,4096]{1,0:T(8,128)(2,1)} %fusion.8.normed, bf16[128,4096]{1,0:T(8,128)(2,1)} %copy-done, bf16[8,64,128]{2,1,0:T(8,128)(2,1)} %fusion.16.pick, bf16[8,128,64]{2,1,0:T(8,128)(2,1)} %fusion.14.pick_back, f32[512,1]{1,0:T(8,128)} %reshape.127.slot_weight, bf16[704,4096]{1,0:T(8,128)(2,1)} %bitcast.35, ...), custom_call_target="tpu_custom_call" | custom-call | tf_op jit(solution)/shard_map/pallas_call | solution.py:319
  175.1 2.3 %copy.25 = bf16[128,4096]{1,0:T(8,128)(2,1)} copy(bf16[128,4096]{1,0:T(8,128)(2,1)} %shard_map.129) | data formatting | bytes 2097152
  (31 shorter events, 0.5 us)
Async XLA Ops:
  46.5 3.0 %copy-start.5 = (bf16[1024,512]{1,0:T(8,128)(2,1)S(1)}, bf16[1024,512]{1,0:T(8,128)(2,1)}, u32[]{:S(2)}) copy-start(bf16[1024,512]{1,0:T(8,128)(2,1)} %get-tuple-element.12) | copy-start | bytes 3145732
  49.5 19.0 %copy-start.1 = (bf16[128,4096]{1,0:T(8,128)(2,1)S(1)}, bf16[128,4096]{1,0:T(8,128)(2,1)}, u32[]{:S(2)}) copy-start(bf16[128,4096]{1,0:T(8,128)(2,1)} %param.16) | copy-start | bytes 3145732
  49.5 19.0 %copy-start.3 = (f32[4096]{0:T(1024)S(1)}, f32[4096]{0:T(1024)}, u32[]{:S(2)}) copy-start(f32[4096]{0:T(1024)} %param.19) | copy-start | bytes 49156
  52.0 19.5 %copy-start.4 = (f32[4096]{0:T(1024)S(1)}, f32[4096]{0:T(1024)}, u32[]{:S(2)}) copy-start(f32[4096]{0:T(1024)} %param.20) | copy-start | bytes 49156
  52.0 20.8 %copy-start.2 = (f32[8,8,128]{2,1,0:T(8,128)S(1)}, f32[8,8,128]{2,1,0:T(8,128)}, u32[]{:S(2)}) copy-start(f32[8,8,128]{2,1,0:T(8,128)} %get-tuple-element.9) | copy-start | bytes 98308
  70.5 1.0 copy-start
where the time goes:
time: 178 us; the launch traced here: 177 us
  Pallas kernels  153 us (86%)
  other arithmetic  11.9 us (7%)
  local copies, waits for them, and re-layouts  6.64 us (4%)
  matrix products  5.41 us (3%)
    pallas_call x1, Pallas kernels, cube_experts(): pl.pallas_call(expert_kernel, out_shape=jax.ShapeDtypeStruct((tokens, mod...  98.9 us
    pallas_call x2, Pallas kernels, exchange(): pl.pallas_call(functools.partial(exchange_kernel, moves, devices), out_sh...  54.4 us
    unnamed x14, local copies, waits for them, and re-layouts  4.07 us

commit v1 on v0

v1 whole, which is shorter than its diff:
```python
import functools
import math

import jax
import jax.numpy as jnp
from jax import lax
from jax.experimental import pallas as pl
from jax.experimental.pallas import tpu as pltpu
from jax.sharding import PartitionSpec as P

EPSILON = 1e-06
CHUNKS = 4
HALVES = 2
FLIPS = (6, 4, 2, 7, 5, 3, 1)
SLOT_ORDER = (0, 2, 4, 6, 1, 3, 5, 7)
VMEM_BYTES = 67043328
LOW = -1e30


def exchange_kernel(moves, devices, *refs):
    count = len(moves)
    sources, targets = refs[:count], refs[count : 2 * count]
    send_sem, recv_sem, local_sem = refs[2 * count :]
    me = lax.axis_index("seq")
    others = [lax.rem(me + step, devices) for step in range(1, devices)]
    barrier = pltpu.get_barrier_semaphore()
    for other in others:
        pl.semaphore_signal(
            barrier, inc=1, device_id={"seq": other}, device_id_type=pl.DeviceIdType.MESH
        )
    pl.semaphore_wait(barrier, devices - 1)
    copies = []
    for i, (take, put) in enumerate(moves):
        for step, other in enumerate(others):
            copies.append(
                pltpu.make_async_remote_copy(
                    src_ref=take(sources[i], other),
                    dst_ref=put(targets[i], me),
                    send_sem=send_sem.at[i, step],
                    recv_sem=recv_sem.at[i, step],
                    device_id={"seq": other},
                    device_id_type=pl.DeviceIdType.MESH,
                )
            )
            copies[-1].start()
    for i, (take, put) in enumerate(moves):
        copies.append(
            pltpu.make_async_copy(take(sources[i], me), put(targets[i], me), local_sem.at[i])
        )
        copies[-1].start()
    for copy in copies:
        copy.wait()


def exchange(moves, devices, number, sources, shapes):
    far = pl.BlockSpec(memory_space=pl.ANY)
    count = len(moves)
    return pl.pallas_call(
        functools.partial(exchange_kernel, moves, devices),
        out_shape=shapes,
        in_specs=[far] * count,
        out_specs=[far] * count,
        scratch_shapes=[
            pltpu.SemaphoreType.DMA((count, devices - 1)),
            pltpu.SemaphoreType.DMA((count, devices - 1)),
            pltpu.SemaphoreType.DMA((count,)),
        ],
        compiler_params=pltpu.CompilerParams(collective_id=number, has_side_effects=True),
    )(*sources)


def head_mix(query, key, value, input_gate, forget_gate):
    positions, head_dim = query.shape
    cumul_log = jnp.cumsum(jax.nn.log_sigmoid(forget_gate))
    level = input_gate - cumul_log
    top = lax.cummax(level, axis=0)
    scores = lax.dot_general(
        query, key, (((1,), (1,)), ((), ())), preferred_element_type=jnp.float32
    )
    causal = jnp.arange(positions)[:, None] >= jnp.arange(positions)[None, :]
    decay = jnp.exp(jnp.minimum(level[None, :] - top[:, None], 0.0))
    coef = jnp.where(causal, decay * scores, 0.0) * (1.0 / math.sqrt(head_dim))
    denom_sum = jnp.sum(coef, axis=1, keepdims=True)
    numer_sum = jnp.dot(coef.astype(jnp.bfloat16), value, preferred_element_type=jnp.float32)
    return numer_sum / jnp.maximum(jnp.abs(denom_sum), 1.0)


def fused_kernel(
    query_far,
    key_far,
    value_far,
    residual_far,
    input_gate,
    forget_gate,
    routes,
    weights,
    mix_gain,
    ffn_gain,
    gate_far,
    up_far,
    down_far,
    out,
    info,
    gates,
    level,
    top,
    slot_weight,
    query_all,
    key_all,
    value_all,
    mixed,
    mixer_in,
    residual,
    updated,
    rows,
    gate,
    up,
    down,
    gate_sum,
    up_sum,
    hidden,
    own,
    core_out,
    core_in,
    hop_out,
    hop_in,
    keep,
    last_out,
    last_in,
    load_sem,
    info_send,
    info_recv,
    key_send,
    key_recv,
    value_send,
    value_recv,
    query_send,
    query_recv,
    mixed_send,
    mixed_recv,
    gather_send,
    gather_recv,
    core_send,
    core_recv,
    hop_send,
    hop_recv,
    last_send,
    last_recv,
):
    me = lax.axis_index("seq")
    heads, tokens = input_gate.shape
    devices = heads
    head_dim = key_all.shape[1]
    part = tokens // CHUNKS
    width = out.shape[1] // HALVES
    four = devices // 2 * part

    def peer(flip):
        total = 0
        for bit in (1, 2, 4):
            own_bit = lax.rem(lax.div(me, bit), 2)
            total = total + bit * ((1 - own_bit) if flip & bit else own_bit)
        return total

    started = []

    def remote(source, target, send_sem, recv_sem, flip):
        copy = pltpu.make_async_remote_copy(
            src_ref=source,
            dst_ref=target,
            send_sem=send_sem,
            recv_sem=recv_sem,
            device_id={"seq": peer(flip)},
            device_id_type=pl.DeviceIdType.MESH,
        )
        started.append(copy)
        copy.start()
        return copy

    def block_rows(origin, count):
        return pl.ds(pl.multiple_of(origin * count, count), count)

    def head_columns(origin):
        return pl.ds(pl.multiple_of(origin * head_dim, head_dim), head_dim)

    loads = [
        pltpu.make_async_copy(source, target, load_sem.at[i])
        for i, (source, target) in enumerate(
            (
                (key_far.at[:, head_columns(me)], key_all.at[block_rows(me, tokens), :]),
                (value_far.at[:, head_columns(me)], value_all.at[block_rows(me, tokens), :]),
                (residual_far, residual),
                (gate_far, gate),
                (up_far, up),
                (down_far, down),
            )
            + tuple(
                (
                    query_far.at[pl.ds(j * part, part), head_columns(me)],
                    query_all.at[j, block_rows(me, part), :],
                )
                for j in range(CHUNKS)
            )
        )
    ]
    forget = forget_gate[...]
    info[me, 0:8, :] = input_gate[...]
    info[me, 8:16, :] = -(jnp.maximum(-forget, 0.0) + jnp.log1p(jnp.exp(-jnp.abs(forget))))
    info[me, 16:18, :] = routes[...].astype(jnp.float32)
    info[me, 18:20, :] = weights[...]
    barrier = pltpu.get_barrier_semaphore()
    for flip in FLIPS:
        pl.semaphore_signal(
            barrier,
            inc=1,
            device_id={"seq": peer(flip)},
            device_id_type=pl.DeviceIdType.MESH,
        )
    pl.semaphore_wait(barrier, devices - 1)

    infos, keys, values, queries, results = {}, {}, {}, {}, {}
    for flip in FLIPS:
        keys[flip] = remote(
            key_far.at[:, head_columns(peer(flip))],
            key_all.at[block_rows(me, tokens), :],
            key_send.at[flip - 1],
            key_recv.at[flip - 1],
            flip,
        )
        infos[flip] = remote(
            info.at[me], info.at[me], info_send.at[flip - 1], info_recv.at[flip - 1], flip
        )
    for flip in FLIPS:
        values[flip] = remote(
            value_far.at[:, head_columns(peer(flip))],
            value_all.at[block_rows(me, tokens), :],
            value_send.at[flip - 1],
            value_recv.at[flip - 1],
            flip,
        )
    for j in range(CHUNKS):
        for flip in FLIPS:
            queries[j, flip] = remote(
                query_far.at[pl.ds(j * part, part), head_columns(peer(flip))],
                query_all.at[j, block_rows(me, part), :],
                query_send.at[j, flip - 1],
                query_recv.at[j, flip - 1],
                flip,
            )
    for load in loads:
        load.start()

    for flip in FLIPS:
        infos[flip].wait_recv()
    for block in range(devices):
        gates[block : block + 1, :] = info[block, pl.ds(me, 1), :]
        gates[devices + block : devices + block + 1, :] = info[block, pl.ds(heads + me, 1), :]
    across = lax.broadcasted_iota(jnp.int32, (tokens, tokens), 0)
    along = lax.broadcasted_iota(jnp.int32, (tokens, tokens), 1)
    local_sum = jnp.dot(
        gates[devices : 2 * devices, :],
        (across <= along).astype(jnp.float32),
        precision=lax.Precision.HIGHEST,
        preferred_element_type=jnp.float32,
    )
    before = jnp.zeros((1, 1), jnp.float32)
    peak = jnp.full((1, 1), LOW, jnp.float32)
    for block in range(devices):
        line = local_sum[block : block + 1, :]
        level_line = gates[block : block + 1, :] - (line + before)
        before = before + line[:, tokens - 1 : tokens]
        level[:, block * tokens : (block + 1) * tokens] = level_line
        spread = jnp.where(along <= across, jnp.broadcast_to(level_line, (tokens, tokens)), LOW)
        tops = jnp.maximum(jnp.max(spread, axis=1, keepdims=True), peak)
        peak = jnp.maximum(peak, jnp.max(level_line, axis=1, keepdims=True))
        for j in range(CHUNKS):
            top[j, block * part : (block + 1) * part, :] = tops[j * part : (j + 1) * part, :]
    for slot in range(devices):
        told = info.at[peer(slot)] if slot else info.at[me]
        line = jnp.where(told[16:17, :].astype(jnp.int32) == me, told[18:19, :], 0.0) + jnp.where(
            told[17:18, :].astype(jnp.int32) == me, told[19:20, :], 0.0
        )
        spread = jnp.where(along == across, jnp.broadcast_to(line, (tokens, tokens)), 0.0)
        column = jnp.sum(spread, axis=1, keepdims=True)
        place = SLOT_ORDER.index(slot) * part
        for j in range(CHUNKS):
            slot_weight[j, place : place + part, :] = column[j * part : (j + 1) * part, :]

    for flip in FLIPS:
        keys[flip].wait_recv()
        values[flip].wait_recv()
    loads[0].wait()
    loads[1].wait()
    place_in = lax.broadcasted_iota(jnp.int32, (devices * part, 1), 0)
    place_in = lax.shift_right_logical(place_in, part.bit_length() - 1) * (tokens - part) + place_in
    place_key = lax.broadcasted_iota(jnp.int32, (1, devices * tokens), 1)
    for j in range(CHUNKS):
        for flip in FLIPS:
            queries[j, flip].wait_recv()
        loads[6 + j].wait()
        scores = lax.dot_general(
            query_all[j],
            key_all[...],
            (((1,), (1,)), ((), ())),
            preferred_element_type=jnp.float32,
        )
        decay = jnp.exp(jnp.minimum(level[...] - top[j], 0.0))
        coef = jnp.where(place_key <= place_in + j * part, decay * scores, 0.0) * (
            1.0 / math.sqrt(head_dim)
        )
        denom_sum = jnp.sum(coef, axis=1, keepdims=True)
        numer_sum = jnp.dot(
            coef.astype(jnp.bfloat16), value_all[...], preferred_element_type=jnp.float32
        )
        mixed[j] = (numer_sum / jnp.maximum(jnp.abs(denom_sum), 1.0)).astype(jnp.bfloat16)
        for flip in FLIPS:
            results[j, flip] = remote(
                mixed.at[j, block_rows(peer(flip), part), :],
                mixer_in.at[j, :, head_columns(me)],
                mixed_send.at[j, flip - 1],
                mixed_recv.at[j, flip - 1],
                flip,
            )
        mixer_in[j, :, head_columns(me)] = mixed[j, block_rows(me, part), :]

    def slot_rows(slot):
        return pl.ds(SLOT_ORDER.index(slot) * part, part)

    def columns(half):
        return pl.ds(half * width, width)

    gathers = {}

    def gather(j, number, source, target, flip, half=None):
        view = slice(None) if half is None else columns(half)
        gathers[j, number] = remote(
            rows.at[j, slot_rows(source), view],
            rows.at[j, slot_rows(target), view],
            gather_send.at[j, number],
            gather_recv.at[j, number],
            flip,
        )

    def normalise(j):
        for flip in FLIPS:
            results[j, flip].wait_recv()
        if j == 0:
            loads[2].wait()
        span = slice(j * part, (j + 1) * part)
        mixer_out = mixer_in[j].astype(jnp.float32)
        square = jnp.mean(mixer_out * mixer_out, axis=1, keepdims=True)
        value = (
            residual[span, :].astype(jnp.float32)
            + mixer_out * lax.rsqrt(square + EPSILON) * mix_gain[...]
        ).astype(jnp.bfloat16)
        updated[span, :] = value
        value = value.astype(jnp.float32)
        square = jnp.mean(value * value, axis=1, keepdims=True)
        rows[j, 0:part, :] = (value * lax.rsqrt(square + EPSILON) * ffn_gain[...]).astype(
            jnp.bfloat16
        )

    def send_own(j):
        gather(j, 0, 0, 2, 2, 0)
        gather(j, 1, 0, 4, 4, 1)
        gather(j, 2, 0, 2, 2, 1)
        gather(j, 3, 0, 4, 4, 0)
        gather(j, 4, 0, 1, 1)

    def relay(j):
        gathers[j, 0].wait_recv()
        gather(j, 5, 2, 6, 4, 0)
        gathers[j, 1].wait_recv()
        gather(j, 6, 4, 6, 2, 1)
        gathers[j, 2].wait_recv()
        gather(j, 7, 2, 3, 1)
        gathers[j, 3].wait_recv()
        gather(j, 8, 4, 5, 1)

    def relay_last(j):
        gathers[j, 5].wait_recv()
        gathers[j, 6].wait_recv()
        gather(j, 9, 6, 7, 1)

    core_copies, hop_copies, last_copies = {}, {}, {}

    def compute(j):
        for number in (4, 7, 8, 9):
            gathers[j, number].wait_recv()
        if j == 0:
            loads[3].wait()
            loads[4].wait()
        for weight, total in ((gate, gate_sum), (up, up_sum)):
            total[...] = lax.dot_general(
                rows[j],
                weight[...],
                (((1,), (1,)), ((), ())),
                preferred_element_type=jnp.float32,
            )
        gate_val = gate_sum[...]
        hidden[...] = (gate_val / (1.0 + jnp.exp(-gate_val)) * up_sum[...]).astype(jnp.bfloat16)
        if j == 0:
            loads[5].wait()
        for half in range(HALVES):
            terms = (
                jnp.dot(hidden[...], down[:, columns(half)], preferred_element_type=jnp.float32)
                * slot_weight[j]
            ).astype(jnp.bfloat16)
            own[j % 2, half] = terms[:four, :]
            core_out[j, half] = terms[four:, :]
            core_copies[j, half] = remote(
                core_out.at[j, half],
                core_in.at[j, half],
                core_send.at[j, half],
                core_recv.at[j, half],
                1,
            )

    def first_hop(j, half):
        first, second = (2, 4) if half == 0 else (4, 2)
        core_copies[j, half].wait_recv()
        for slot in (6, first, second, 0):
            view = slot_rows(slot)
            both = own[j % 2, half, view, :].astype(jnp.float32) + core_in[
                j, half, view, :
            ].astype(jnp.float32)
            if slot in (0, second):
                keep[j, half, 0 if slot == 0 else 1] = both
                continue
            place = 1 if slot == 6 else 0
            hop_out[j, half, place] = both.astype(jnp.bfloat16)
            hop_copies[j, half, place] = remote(
                hop_out.at[j, half, place],
                hop_in.at[j, half, place],
                hop_send.at[j, half, place],
                hop_recv.at[j, half, place],
                first,
            )

    def second_hop(j, half):
        second = 4 if half == 0 else 2
        hop_copies[j, half, 1].wait_recv()
        last_out[j, half] = (
            keep[j, half, 1] + hop_in[j, half, 1].astype(jnp.float32)
        ).astype(jnp.bfloat16)
        last_copies[j, half] = remote(
            last_out.at[j, half],
            last_in.at[j, half],
            last_send.at[j, half],
            last_recv.at[j, half],
            second,
        )

    def finish(j, half):
        hop_copies[j, half, 0].wait_recv()
        last_copies[j, half].wait_recv()
        span = slice(j * part, (j + 1) * part)
        out[span, columns(half)] = (
            updated[span, columns(half)].astype(jnp.float32)
            + (
                keep[j, half, 0]
                + hop_in[j, half, 0].astype(jnp.float32)
                + last_in[j, half].astype(jnp.float32)
            )
        ).astype(jnp.bfloat16)

    def both_halves(step, j):
        for half in range(HALVES):
            step(j, half)

    normalise(0)
    send_own(0)
    normalise(1)
    send_own(1)
    normalise(2)
    normalise(3)
    relay(0)
    send_own(2)
    relay(1)
    send_own(3)
    relay_last(0)
    compute(0)
    relay(2)
    relay_last(1)
    both_halves(first_hop, 0)
    compute(1)
    relay(3)
    relay_last(2)
    both_halves(first_hop, 1)
    both_halves(second_hop, 0)
    compute(2)
    relay_last(3)
    both_halves(first_hop, 2)
    both_halves(second_hop, 1)
    both_halves(finish, 0)
    compute(3)
    both_halves(first_hop, 3)
    both_halves(second_hop, 2)
    both_halves(finish, 1)
    both_halves(second_hop, 3)
    both_halves(finish, 2)
    both_halves(finish, 3)
    for copy in started:
        copy.wait_send()


def fused_block(*operands):
    queries, gates, gate_weight = operands[0], operands[4], operands[10]
    tokens, model_width = queries.shape
    devices = gates.shape[0]
    head_dim = model_width // devices
    hidden_width = gate_weight.shape[0]
    part = tokens // CHUNKS
    width = model_width // HALVES
    batch = devices * part
    near = pl.BlockSpec(memory_space=pltpu.VMEM)
    far = pl.BlockSpec(memory_space=pl.ANY)

    def space(*shape, kind=jnp.bfloat16):
        return pltpu.VMEM(shape, kind)

    def flags(*shape):
        return [pltpu.SemaphoreType.DMA(shape)] * 2

    return pl.pallas_call(
        fused_kernel,
        out_shape=jax.ShapeDtypeStruct((tokens, model_width), jnp.bfloat16),
        in_specs=[far] * 4 + [near] * 6 + [far] * 3,
        out_specs=near,
        scratch_shapes=[
            space(devices, 24, tokens, kind=jnp.float32),
            space(2 * devices, tokens, kind=jnp.float32),
            space(1, devices * tokens, kind=jnp.float32),
            space(CHUNKS, batch, 1, kind=jnp.float32),
            space(CHUNKS, batch, 1, kind=jnp.float32),
            space(CHUNKS, batch, head_dim),
            space(devices * tokens, head_dim),
            space(devices * tokens, head_dim),
            space(CHUNKS, batch, head_dim),
            space(CHUNKS, part, model_width),
            space(tokens, model_width),
            space(tokens, model_width),
            space(CHUNKS, batch, model_width),
            space(*gate_weight.shape),
            space(*gate_weight.shape),
            space(*gate_weight.shape),
            space(batch, hidden_width, kind=jnp.float32),
            space(batch, hidden_width, kind=jnp.float32),
            space(batch, hidden_width),
            space(2, HALVES, batch // 2, width),
            space(CHUNKS, HALVES, batch // 2, width),
            space(CHUNKS, HALVES, batch // 2, width),
            space(CHUNKS, HALVES, 2, part, width),
            space(CHUNKS, HALVES, 2, part, width),
            space(CHUNKS, HALVES, 2, part, width, kind=jnp.float32),
            space(CHUNKS, HALVES, part, width),
            space(CHUNKS, HALVES, part, width),
            pltpu.SemaphoreType.DMA((6 + CHUNKS,)),
        ]
        + flags(devices - 1)
        + flags(devices - 1)
        + flags(devices - 1)
        + flags(CHUNKS, devices - 1)
        + flags(CHUNKS, devices - 1)
        + flags(CHUNKS, 10)
        + flags(CHUNKS, HALVES)
        + flags(CHUNKS, HALVES, 2)
        + flags(CHUNKS, HALVES),
        compiler_params=pltpu.CompilerParams(
            collective_id=1, has_side_effects=True, vmem_limit_bytes=VMEM_BYTES
        ),
    )(*operands)


def shards(
    queries,
    key_vectors,
    value_vectors,
    residual_in,
    input_logit,
    forget_logit,
    mix_gain,
    ffn_gain,
    expert_gate,
    expert_up,
    expert_down,
    routes,
    route_weight,
):
    tokens, model_width = queries.shape
    head_count = input_logit.shape[0]
    head_dim = model_width // head_count
    devices = lax.axis_size("seq")
    group = devices // head_count
    group_width = model_width // devices
    if devices == 8 and head_count == 8:
        return fused_block(
            queries,
            key_vectors,
            value_vectors,
            residual_in,
            input_logit,
            forget_logit,
            jnp.transpose(routes),
            jnp.transpose(route_weight),
            mix_gain.reshape(1, -1),
            ffn_gain.reshape(1, -1),
            jnp.transpose(expert_gate[0]),
            jnp.transpose(expert_up[0]),
            expert_down[0],
        )

    capacity = 4 * tokens // devices
    flat_routes = routes.reshape(-1)
    matches = (flat_routes[:, None] == jnp.arange(devices, dtype=jnp.int32)[None, :]).astype(
        jnp.int32
    )
    before = jnp.cumsum(matches, axis=0) - matches
    position = jnp.sum(before * matches, axis=1)
    position = position.reshape(tokens, 2)
    slot_index = (flat_routes * capacity + position.reshape(-1)).reshape(tokens, 2)
    notes = jnp.stack(
        (jnp.repeat(input_logit, group, axis=0), jnp.repeat(forget_logit, group, axis=0)), axis=1
    )
    def columns_of(width, share):
        return lambda ref, other: ref.at[
            :, pl.ds(pl.multiple_of((other // share) * width, width), width)
        ]

    def rows_from(ref, origin):
        return ref.at[pl.ds(pl.multiple_of(origin * tokens, tokens), tokens), :]

    def entry(ref, other):
        return ref.at[other]

    head_columns = columns_of(head_dim, group)
    own_columns = columns_of(group_width, 1)
    tall = devices * tokens
    told, key_all, query_all, value_all = exchange(
        (
            (entry, entry),
            (head_columns, rows_from),
            (head_columns, rows_from),
            (own_columns, rows_from),
        ),
        devices,
        2,
        (notes, key_vectors, queries, value_vectors),
        (
            jax.ShapeDtypeStruct(notes.shape, jnp.float32),
            jax.ShapeDtypeStruct((tall, head_dim), jnp.bfloat16),
            jax.ShapeDtypeStruct((tall, head_dim), jnp.bfloat16),
            jax.ShapeDtypeStruct((tall, group_width), jnp.bfloat16),
        ),
    )
    mixed = head_mix(
        query_all, key_all, value_all, told[:, 0].reshape(-1), told[:, 1].reshape(-1)
    ).astype(jnp.bfloat16)
    (mixer_out,) = exchange(
        ((rows_from, own_columns),),
        devices,
        3,
        (mixed,),
        (jax.ShapeDtypeStruct((tokens, model_width), jnp.bfloat16),),
    )
    mixer_out = mixer_out.astype(jnp.float32)
    mixer_square = jnp.mean(mixer_out * mixer_out, axis=1, keepdims=True)
    updated = (
        residual_in.astype(jnp.float32) + mixer_out * lax.rsqrt(mixer_square + EPSILON) * mix_gain
    ).astype(jnp.bfloat16)
    updated_float = updated.astype(jnp.float32)
    updated_square = jnp.mean(updated_float * updated_float, axis=1, keepdims=True)
    normed = (updated_float * lax.rsqrt(updated_square + EPSILON) * ffn_gain).astype(jnp.bfloat16)
    columns = jnp.arange(devices * capacity, dtype=jnp.int32)
    pick_first = (slot_index[:, 0:1] == columns[None, :]).astype(jnp.bfloat16)
    pick_second = (slot_index[:, 1:2] == columns[None, :]).astype(jnp.bfloat16)
    spread = jnp.einsum(
        "tc,td->cd", pick_first + pick_second, normed, preferred_element_type=jnp.float32
    ).astype(jnp.bfloat16)
    outbound = spread.reshape(devices, capacity, model_width)
    block_in = lax.all_to_all(outbound, "seq", split_axis=0, concat_axis=0, tiled=True)
    row_block = block_in.reshape(-1, model_width)
    gate_val = jnp.dot(row_block, expert_gate[0], preferred_element_type=jnp.float32)
    up_val = jnp.dot(row_block, expert_up[0], preferred_element_type=jnp.float32)
    hidden = (jax.nn.silu(gate_val) * up_val).astype(jnp.bfloat16)
    result = jnp.dot(hidden, expert_down[0], preferred_element_type=jnp.float32).astype(
        jnp.bfloat16
    )
    inbound = lax.all_to_all(
        result.reshape(block_in.shape), "seq", split_axis=0, concat_axis=0, tiled=True
    )
    flat_back = inbound.reshape(devices * capacity, model_width)
    first_out = jnp.dot(pick_first, flat_back, preferred_element_type=jnp.float32)
    second_out = jnp.dot(pick_second, flat_back, preferred_element_type=jnp.float32)
    expert_mix = route_weight[:, 0:1] * first_out + route_weight[:, 1:2] * second_out
    return (updated_float + expert_mix).astype(jnp.bfloat16)


def solution(mesh):
    return jax.shard_map(
        shards,
        mesh=mesh,
        in_specs=(
            P(("batch", "seq"), None),
            P(("batch", "seq"), None),
            P(("batch", "seq"), None),
            P(("batch", "seq"), None),
            P(None, ("batch", "seq")),
            P(None, ("batch", "seq")),
            P(),
            P(),
            P("seq", None, None),
            P("seq", None, None),
            P("seq", None, None),
            P(("batch", "seq"), None),
            P(("batch", "seq"), None),
        ),
        out_specs=P(("batch", "seq"), None),
        check_vma=False,
    )
```

time: 178 us -> 128 us (0.72)
  Pallas kernels: 153 us -> 125 us
  other arithmetic: 11.9 us -> 0 us
  matrix products: 5.41 us -> 0 us
  local copies, waits for them, and re-layouts: 6.64 us -> 2.29 us
    pallas_call x3 -> x1, Pallas kernels: 153 us -> 125 us  [fused_block(): pl.pallas_call(fused_kernel, out_shape=jax.ShapeDtypeStruct((tokens, mode...]
    dot_general x2 -> x0, matrix products: 5.41 us -> none  [the longest x1 2.99 us: head_mix(): lax.dot_general(query, key, (((1,), (1,)), ((), ())), preferred_element_t...]
    convert_element_type x6 -> x0, other arithmetic: 3.76 us -> none  [the longest x2 1.75 us: shards(): pick = jnp.logical_or(pick_one, pick_two).astype(jnp.bfloat16)]
    reduce_sum x4 -> x0, other arithmetic: 3.72 us -> none  [the longest x1 1.96 us: shards(): jnp.mean(updated_float * updated_float, axis=1, keepdims=True)]
    unnamed x14 -> x1, local copies, waits for them, and re-layouts: 4.07 us -> 2.29 us
where the time goes in v1:
time: 128 us
  Pallas kernels  125 us (98%)
  local copies, waits for them, and re-layouts  2.29 us (2%)
    pallas_call x1, Pallas kernels, fused_block(): pl.pallas_call(fused_kernel, out_shape=jax.ShapeDtypeStruct((tokens, mode...  125 us

profile of v1, /device:TPU:0, one launch (start us, length us, event | category | flops | bytes accessed | tf_op | source)
XLA Modules:
  0.0 127.7 jit_solution(2845731816367491639)
XLA Ops:
  0.0 125.4 %shard_map.127 = bf16[128,4096]{1,0:T(8,128)(2,1)} custom-call(bf16[128,4096]{1,0:T(8,128)(2,1)} %query_far.1, bf16[128,4096]{1,0:T(8,128)(2,1)} %key_far.1, bf16[128,4096]{1,0:T(8,128)(2,1)} %value_far.1, bf16[128,4096]{1,0:T(8,128)(2,1)} %residual_far.1, f32[8,128]{1,0:T(8,128)} %input_gate.1, f32[8,128]{1,0:T(8,128)} %forget_gate.1, s32[2,128]{1,0:T(2,128)} %bitcast.16, ...), custom_call_target="tpu_custom_call" | custom-call | tf_op jit(solution)/shard_map/pallas_call | solution.py:525
  125.4 2.3 %copy.15 = bf16[128,4096]{1,0:T(8,128)(2,1)} copy(bf16[128,4096]{1,0:T(8,128)(2,1)} %shard_map.127) | data formatting | bytes 2097152

commit v2 on v1

--- a/solution.py
+++ b/solution.py
@@ -13,7 +13,7 @@
 HALVES = 2
 FLIPS = (6, 4, 2, 7, 5, 3, 1)
 SLOT_ORDER = (0, 2, 4, 6, 1, 3, 5, 7)
-VMEM_BYTES = 67043328
+VMEM_BYTES = 64 * 1024 * 1024 - 2 * 1024 * 1024
 LOW = -1e30
 
 
@@ -90,16 +90,22 @@
     key_far,
     value_far,
     residual_far,
+    input_far,
+    forget_far,
+    routes_far,
+    weights_far,
+    mix_far,
+    ffn_far,
+    gate_far,
+    up_far,
+    down_far,
+    out,
     input_gate,
     forget_gate,
     routes,
     weights,
     mix_gain,
     ffn_gain,
-    gate_far,
-    up_far,
-    down_far,
-    out,
     info,
     gates,
     level,
@@ -162,7 +168,8 @@
             total = total + bit * ((1 - own_bit) if flip & bit else own_bit)
         return total
 
-    started = []
+    def arrive(whole, flag):
+        pltpu.make_async_copy(whole, whole, flag).wait()
 
     def remote(source, target, send_sem, recv_sem, flip):
         copy = pltpu.make_async_remote_copy(
@@ -173,7 +180,6 @@
             device_id={"seq": peer(flip)},
             device_id_type=pl.DeviceIdType.MESH,
         )
-        started.append(copy)
         copy.start()
         return copy
 
@@ -183,6 +189,14 @@
     def head_columns(origin):
         return pl.ds(pl.multiple_of(origin * head_dim, head_dim), head_dim)
 
+    barrier = pltpu.get_barrier_semaphore()
+    for flip in FLIPS:
+        pl.semaphore_signal(
+            barrier,
+            inc=1,
+            device_id={"seq": peer(flip)},
+            device_id_type=pl.DeviceIdType.MESH,
+        )
     loads = [
         pltpu.make_async_copy(source, target, load_sem.at[i])
         for i, (source, target) in enumerate(
@@ -201,57 +215,59 @@
                 )
                 for j in range(CHUNKS)
             )
+            + (
+                (input_far, input_gate),
+                (forget_far, forget_gate),
+                (routes_far, routes),
+                (weights_far, weights),
+                (mix_far, mix_gain),
+                (ffn_far, ffn_gain),
+            )
         )
     ]
+    for load in loads[-6:] + loads[:3] + loads[6:-6]:
+        load.start()
+    for load in loads[-6:]:
+        load.wait()
     forget = forget_gate[...]
     info[me, 0:8, :] = input_gate[...]
     info[me, 8:16, :] = -(jnp.maximum(-forget, 0.0) + jnp.log1p(jnp.exp(-jnp.abs(forget))))
     info[me, 16:18, :] = routes[...].astype(jnp.float32)
     info[me, 18:20, :] = weights[...]
-    barrier = pltpu.get_barrier_semaphore()
+    pl.semaphore_wait(barrier, devices - 1)
+
     for flip in FLIPS:
-        pl.semaphore_signal(
-            barrier,
-            inc=1,
-            device_id={"seq": peer(flip)},
-            device_id_type=pl.DeviceIdType.MESH,
-        )
-    pl.semaphore_wait(barrier, devices - 1)
-
-    infos, keys, values, queries, results = {}, {}, {}, {}, {}
-    for flip in FLIPS:
-        keys[flip] = remote(
+        remote(
             key_far.at[:, head_columns(peer(flip))],
             key_all.at[block_rows(me, tokens), :],
-            key_send.at[flip - 1],
-            key_recv.at[flip - 1],
+            key_send.at[0],
+            key_recv.at[0],
             flip,
         )
-        infos[flip] = remote(
-            info.at[me], info.at[me], info_send.at[flip - 1], info_recv.at[flip - 1], flip
+        remote(
+            info.at[me], info.at[me], info_send.at[0], info_recv.at[0], flip
         )
     for flip in FLIPS:
-        values[flip] = remote(
+        remote(
             value_far.at[:, head_columns(peer(flip))],
             value_all.at[block_rows(me, tokens), :],
-            value_send.at[flip - 1],
-            value_recv.at[flip - 1],
+            value_send.at[0],
+            value_recv.at[0],
             flip,
         )
     for j in range(CHUNKS):
         for flip in FLIPS:
-            queries[j, flip] = remote(
+            remote(
                 query_far.at[pl.ds(j * part, part), head_columns(peer(flip))],
                 query_all.at[j, block_rows(me, part), :],
-                query_send.at[j, flip - 1],
-                query_recv.at[j, flip - 1],
+                query_send.at[0],
+                query_recv.at[j],
                 flip,
             )
-    for load in loads:
+    for load in loads[3:6]:
         load.start()
 
-    for flip in FLIPS:
-        infos[flip].wait_recv()
+    arrive(info.at[1:], info_recv.at[0])
     for block in range(devices):
         gates[block : block + 1, :] = info[block, pl.ds(me, 1), :]
         gates[devices + block : devices + block + 1, :] = info[block, pl.ds(heads + me, 1), :]
@@ -286,17 +302,15 @@
         for j in range(CHUNKS):
             slot_weight[j, place : place + part, :] = column[j * part : (j + 1) * part, :]
 
-    for flip in FLIPS:
-        keys[flip].wait_recv()
-        values[flip].wait_recv()
+    arrive(key_all.at[tokens:, :], key_recv.at[0])
+    arrive(value_all.at[tokens:, :], value_recv.at[0])
     loads[0].wait()
     loads[1].wait()
     place_in = lax.broadcasted_iota(jnp.int32, (devices * part, 1), 0)
     place_in = lax.shift_right_logical(place_in, part.bit_length() - 1) * (tokens - part) + place_in
     place_key = lax.broadcasted_iota(jnp.int32, (1, devices * tokens), 1)
     for j in range(CHUNKS):
-        for flip in FLIPS:
-            queries[j, flip].wait_recv()
+        arrive(query_all.at[j, part:, :], query_recv.at[j])
         loads[6 + j].wait()
         scores = lax.dot_general(
             query_all[j],
@@ -314,11 +328,11 @@
         )
         mixed[j] = (numer_sum / jnp.maximum(jnp.abs(denom_sum), 1.0)).astype(jnp.bfloat16)
         for flip in FLIPS:
-            results[j, flip] = remote(
+            remote(
                 mixed.at[j, block_rows(peer(flip), part), :],
                 mixer_in.at[j, :, head_columns(me)],
-                mixed_send.at[j, flip - 1],
-                mixed_recv.at[j, flip - 1],
+                mixed_send.at[0],
+                mixed_recv.at[j],
                 flip,
             )
         mixer_in[j, :, head_columns(me)] = mixed[j, block_rows(me, part), :]
@@ -336,14 +350,13 @@
         gathers[j, number] = remote(
             rows.at[j, slot_rows(source), view],
             rows.at[j, slot_rows(target), view],
-            gather_send.at[j, number],
+            gather_send.at[0],
             gather_recv.at[j, number],
             flip,
         )
 
     def normalise(j):
-        for flip in FLIPS:
-            results[j, flip].wait_recv()
+        arrive(mixer_in.at[j, :, head_dim:], mixed_recv.at[j])
         if j == 0:
             loads[2].wait()
         span = slice(j * part, (j + 1) * part)
@@ -411,7 +424,7 @@
             core_copies[j, half] = remote(
                 core_out.at[j, half],
                 core_in.at[j, half],
-                core_send.at[j, half],
+                core_send.at[0],
                 core_recv.at[j, half],
                 1,
             )
@@ -432,7 +445,7 @@
             hop_copies[j, half, place] = remote(
                 hop_out.at[j, half, place],
                 hop_in.at[j, half, place],
-                hop_send.at[j, half, place],
+                hop_send.at[0],
                 hop_recv.at[j, half, place],
                 first,
             )
@@ -446,7 +459,7 @@
         last_copies[j, half] = remote(
             last_out.at[j, half],
             last_in.at[j, half],
-            last_send.at[j, half],
+            last_send.at[0],
             last_recv.at[j, half],
             second,
         )
@@ -500,8 +513,18 @@
     both_halves(second_hop, 3)
     both_halves(finish, 2)
     both_halves(finish, 3)
-    for copy in started:
-        copy.wait_send()
+    for whole, flag in (
+        (info.at[1:], info_send),
+        (key_all.at[tokens:, :], key_send),
+        (value_all.at[tokens:, :], value_send),
+        (query_all.at[:, part:, :], query_send),
+        (mixed.at[:, part:, :], mixed_send),
+        (rows.at[:, part:, :], gather_send),
+        (core_out, core_send),
+        (hop_out, hop_send),
+        (last_out, last_send),
+    ):
+        arrive(whole, flag.at[0])
 
 
 def fused_block(*operands):
@@ -520,14 +543,20 @@
         return pltpu.VMEM(shape, kind)
 
     def flags(*shape):
-        return [pltpu.SemaphoreType.DMA(shape)] * 2
+        return [pltpu.SemaphoreType.DMA((1,)), pltpu.SemaphoreType.DMA(shape)]
 
     return pl.pallas_call(
         fused_kernel,
-        out_shape=jax.ShapeDtypeStruct((tokens, model_width), jnp.bfloat16),
-        in_specs=[far] * 4 + [near] * 6 + [far] * 3,
+        out_shape=pltpu.VMEM((tokens, model_width), jnp.bfloat16),
+        in_specs=[far] * 13,
         out_specs=near,
         scratch_shapes=[
+            space(devices, tokens, kind=jnp.float32),
+            space(devices, tokens, kind=jnp.float32),
+            space(2, tokens, kind=jnp.int32),
+            space(2, tokens, kind=jnp.float32),
+            space(1, model_width, kind=jnp.float32),
+            space(1, model_width, kind=jnp.float32),
             space(devices, 24, tokens, kind=jnp.float32),
             space(2 * devices, tokens, kind=jnp.float32),
             space(1, devices * tokens, kind=jnp.float32),
@@ -555,13 +584,13 @@
             space(CHUNKS, HALVES, 2, part, width, kind=jnp.float32),
             space(CHUNKS, HALVES, part, width),
             space(CHUNKS, HALVES, part, width),
-            pltpu.SemaphoreType.DMA((6 + CHUNKS,)),
+            pltpu.SemaphoreType.DMA((12 + CHUNKS,)),
         ]
-        + flags(devices - 1)
-        + flags(devices - 1)
-        + flags(devices - 1)
-        + flags(CHUNKS, devices - 1)
-        + flags(CHUNKS, devices - 1)
+        + flags(1)
+        + flags(1)
+        + flags(1)
+        + flags(CHUNKS)
+        + flags(CHUNKS)
         + flags(CHUNKS, 10)
         + flags(CHUNKS, HALVES)
         + flags(CHUNKS, HALVES, 2)

time: 128 us -> 123 us (0.961)
  Pallas kernels: 125 us -> 122 us
  local copies, waits for them, and re-layouts: 2.29 us -> 0.97 us
    pallas_call x1, Pallas kernels: 125 us -> 122 us  [fused_block(): pl.pallas_call(fused_kernel, out_shape=pltpu.VMEM((tokens, model_width),...]
    unnamed x1, local copies, waits for them, and re-layouts: 2.29 us -> 0.97 us
where the time goes in v2:
time: 123 us; the launch traced here: 122 us
  Pallas kernels  122 us (99%)
    pallas_call x1, Pallas kernels, fused_block(): pl.pallas_call(fused_kernel, out_shape=pltpu.VMEM((tokens, model_width),...  122 us

profile of v2, /device:TPU:0, one launch (start us, length us, event | category | flops | bytes accessed | tf_op | source)
XLA Modules:
  0.0 122.5 jit_solution(7090968226670713130)
XLA Ops:
  0.0 121.5 %shard_map.127 = bf16[128,4096]{1,0:T(8,128)(2,1)S(1)} custom-call(bf16[128,4096]{1,0:T(8,128)(2,1)} %query_far.1, bf16[128,4096]{1,0:T(8,128)(2,1)} %key_far.1, bf16[128,4096]{1,0:T(8,128)(2,1)} %value_far.1, bf16[128,4096]{1,0:T(8,128)(2,1)} %residual_far.1, f32[8,128]{1,0:T(8,128)} %input_far.1, f32[8,128]{1,0:T(8,128)} %forget_far.1, s32[2,128]{1,0:T(2,128)} %bitcast.16, ...), custom_call_target="tpu_custom_call" | custom-call | tf_op jit(solution)/shard_map/pallas_call | solution.py:548
  121.5 1.0 copy.15

commit v3 on v2

--- a/solution.py
+++ b/solution.py
@@ -13,7 +13,7 @@
 HALVES = 2
 FLIPS = (6, 4, 2, 7, 5, 3, 1)
 SLOT_ORDER = (0, 2, 4, 6, 1, 3, 5, 7)
-VMEM_BYTES = 64 * 1024 * 1024 - 2 * 1024 * 1024
+VMEM_BYTES = 64 * 1024 * 1024 - 1280 * 1024
 LOW = -1e30
 
 
@@ -107,16 +107,25 @@
     mix_gain,
     ffn_gain,
     info,
-    gates,
     level,
+    peak_before,
+    key_level,
     top,
     slot_weight,
-    query_all,
-    key_all,
-    value_all,
+    query_wide,
+    query_slim,
+    key_wide,
+    value_wide,
+    key_slim,
+    value_slim,
+    reply_wide,
+    reply_slim,
+    from_far_row,
+    from_near_wide,
+    from_near_slim,
+    denom,
     mixed,
     mixer_in,
-    residual,
     updated,
     rows,
     gate,
@@ -134,14 +143,16 @@
     last_out,
     last_in,
     load_sem,
-    info_send,
-    info_recv,
-    key_send,
-    key_recv,
-    value_send,
-    value_recv,
-    query_send,
-    query_recv,
+    info_sem,
+    pair_send,
+    pair_recv,
+    far_sem,
+    wide_send,
+    wide_recv,
+    slim_send,
+    slim_recv,
+    reply_send,
+    reply_recv,
     mixed_send,
     mixed_recv,
     gather_send,
@@ -156,10 +167,23 @@
     me = lax.axis_index("seq")
     heads, tokens = input_gate.shape
     devices = heads
-    head_dim = key_all.shape[1]
+    model_width = out.shape[1]
+    head_dim = model_width // heads
     part = tokens // CHUNKS
-    width = out.shape[1] // HALVES
+    width = model_width // HALVES
     four = devices // 2 * part
+    slice_width = 2 * head_dim
+    core = lax.rem(me, 2)
+    column = lax.rem(lax.div(me, 2), 2)
+    row = lax.div(me, 4)
+    chip = lax.div(me, 2)
+    chip_x = chip + 1 - 2 * column
+    chip_y = chip + 2 - 4 * row
+    key_chip = chip_x * (1 - row) + chip_y * row
+    query_chip = chip_y * (1 - row) + chip_x * row
+    wide_base = (1 - row) * width
+    slim_base = row * width
+    bases = (wide_base, slim_base)
 
     def peer(flip):
         total = 0
@@ -171,8 +195,8 @@
     def arrive(whole, flag):
         pltpu.make_async_copy(whole, whole, flag).wait()
 
-    def remote(source, target, send_sem, recv_sem, flip):
-        copy = pltpu.make_async_remote_copy(
+    def prepared(source, target, send_sem, recv_sem, flip):
+        return pltpu.make_async_remote_copy(
             src_ref=source,
             dst_ref=target,
             send_sem=send_sem,
@@ -180,14 +204,20 @@
             device_id={"seq": peer(flip)},
             device_id_type=pl.DeviceIdType.MESH,
         )
+
+    def remote(*arguments):
+        copy = prepared(*arguments)
         copy.start()
         return copy
 
-    def block_rows(origin, count):
-        return pl.ds(pl.multiple_of(origin * count, count), count)
-
-    def head_columns(origin):
-        return pl.ds(pl.multiple_of(origin * head_dim, head_dim), head_dim)
+    def span_of(index, count, first=0):
+        return pl.ds(pl.multiple_of(index * count + first, count), count)
+
+    def head_columns(base, owner):
+        return pl.ds(pl.multiple_of(base + owner * slice_width, slice_width), slice_width)
+
+    def core_of(flip):
+        return 1 - core if flip % 2 else core
 
     barrier = pltpu.get_barrier_semaphore()
     for flip in FLIPS:
@@ -197,37 +227,39 @@
             device_id={"seq": peer(flip)},
             device_id_type=pl.DeviceIdType.MESH,
         )
+    small = (
+        (input_far, input_gate),
+        (forget_far, forget_gate),
+        (routes_far, routes),
+        (weights_far, weights),
+        (mix_far, mix_gain),
+        (ffn_far, ffn_gain),
+    )
+    blocks = tuple(
+        (far.at[:, head_columns(base, core)], target.at[span_of(core, tokens), :])
+        for base, far, target in (
+            (wide_base, key_far, key_wide),
+            (wide_base, value_far, value_wide),
+            (slim_base, key_far, key_slim),
+            (slim_base, value_far, value_slim),
+        )
+    ) + tuple(
+        (
+            query_far.at[pl.ds(j * part, part), head_columns(base, core)],
+            target.at[j, span_of(core, part), :],
+        )
+        for j in range(CHUNKS)
+        for base, target in ((wide_base, query_wide), (slim_base, query_slim))
+    )
+    large = ((residual_far, updated), (gate_far, gate), (up_far, up), (down_far, down))
     loads = [
         pltpu.make_async_copy(source, target, load_sem.at[i])
-        for i, (source, target) in enumerate(
-            (
-                (key_far.at[:, head_columns(me)], key_all.at[block_rows(me, tokens), :]),
-                (value_far.at[:, head_columns(me)], value_all.at[block_rows(me, tokens), :]),
-                (residual_far, residual),
-                (gate_far, gate),
-                (up_far, up),
-                (down_far, down),
-            )
-            + tuple(
-                (
-                    query_far.at[pl.ds(j * part, part), head_columns(me)],
-                    query_all.at[j, block_rows(me, part), :],
-                )
-                for j in range(CHUNKS)
-            )
-            + (
-                (input_far, input_gate),
-                (forget_far, forget_gate),
-                (routes_far, routes),
-                (weights_far, weights),
-                (mix_far, mix_gain),
-                (ffn_far, ffn_gain),
-            )
-        )
+        for i, (source, target) in enumerate(small + blocks + large)
     ]
-    for load in loads[-6:] + loads[:3] + loads[6:-6]:
+    small_loads, block_loads, large_loads = loads[:6], loads[6:18], loads[18:]
+    for load in small_loads + block_loads:
         load.start()
-    for load in loads[-6:]:
+    for load in small_loads:
         load.wait()
     forget = forget_gate[...]
     info[me, 0:8, :] = input_gate[...]
@@ -237,105 +269,261 @@
     pl.semaphore_wait(barrier, devices - 1)
 
     for flip in FLIPS:
+        remote(info.at[me], info.at[me], info_sem.at[0], info_sem.at[1], flip)
+
+    @pl.when(row == 0)
+    def send_keys():
+        for far, target in ((key_far, key_wide), (value_far, value_wide)):
+            for flip, base in ((2, wide_base), (4, slim_base), (3, wide_base), (5, slim_base)):
+                remote(
+                    far.at[:, head_columns(base, core_of(flip))],
+                    target.at[span_of(core, tokens, 2 * tokens), :],
+                    far_sem.at[0],
+                    far_sem.at[1],
+                    flip,
+                )
+
+    @pl.when(column == 1)
+    def send_slim_queries():
+        for j in range(CHUNKS):
+            for flip in (2, 3):
+                remote(
+                    query_far.at[pl.ds(j * part, part), head_columns(slim_base, core_of(flip))],
+                    query_slim.at[j, span_of(core, part, 2 * part), :],
+                    slim_send.at[0],
+                    slim_recv.at[j],
+                    flip,
+                )
+
+    @pl.when(row == 1)
+    def send_wide_queries():
+        for j in range(CHUNKS):
+            for flip, base in ((2, wide_base), (4, slim_base), (3, wide_base), (5, slim_base)):
+                remote(
+                    query_far.at[pl.ds(j * part, part), head_columns(base, core_of(flip))],
+                    query_wide.at[j, span_of(core, part, 2 * part), :],
+                    wide_send.at[0],
+                    wide_recv.at[j],
+                    flip,
+                )
+
+    for base, far, target in (
+        (wide_base, key_far, key_wide),
+        (wide_base, value_far, value_wide),
+        (slim_base, key_far, key_slim),
+        (slim_base, value_far, value_slim),
+    ):
         remote(
-            key_far.at[:, head_columns(peer(flip))],
-            key_all.at[block_rows(me, tokens), :],
-            key_send.at[0],
-            key_recv.at[0],
-            flip,
-        )
-        remote(
-            info.at[me], info.at[me], info_send.at[0], info_recv.at[0], flip
-        )
-    for flip in FLIPS:
-        remote(
-            value_far.at[:, head_columns(peer(flip))],
-            value_all.at[block_rows(me, tokens), :],
-            value_send.at[0],
-            value_recv.at[0],
-            flip,
+            far.at[:, head_columns(base, 1 - core)],
+            target.at[span_of(core, tokens), :],
+            pair_send.at[0],
+            pair_recv.at[CHUNKS],
+            1,
         )
     for j in range(CHUNKS):
-        for flip in FLIPS:
+        for base, target in ((wide_base, query_wide), (slim_base, query_slim)):
             remote(
-                query_far.at[pl.ds(j * part, part), head_columns(peer(flip))],
-                query_all.at[j, block_rows(me, part), :],
-                query_send.at[0],
-                query_recv.at[j],
-                flip,
-            )
-    for load in loads[3:6]:
+                query_far.at[pl.ds(j * part, part), head_columns(base, 1 - core)],
+                target.at[j, span_of(core, part), :],
+                pair_send.at[1],
+                pair_recv.at[j],
+                1,
+            )
+    for load in large_loads:
         load.start()
 
-    arrive(info.at[1:], info_recv.at[0])
-    for block in range(devices):
-        gates[block : block + 1, :] = info[block, pl.ds(me, 1), :]
-        gates[devices + block : devices + block + 1, :] = info[block, pl.ds(heads + me, 1), :]
+    arrive(info.at[1:], info_sem.at[1])
     across = lax.broadcasted_iota(jnp.int32, (tokens, tokens), 0)
     along = lax.broadcasted_iota(jnp.int32, (tokens, tokens), 1)
     local_sum = jnp.dot(
-        gates[devices : 2 * devices, :],
+        info[:, 8:16, :].reshape(devices * heads, tokens),
         (across <= along).astype(jnp.float32),
         precision=lax.Precision.HIGHEST,
         preferred_element_type=jnp.float32,
     )
-    before = jnp.zeros((1, 1), jnp.float32)
-    peak = jnp.full((1, 1), LOW, jnp.float32)
+    before = jnp.zeros((heads, 1), jnp.float32)
+    peak = jnp.full((heads, 1), LOW, jnp.float32)
     for block in range(devices):
-        line = local_sum[block : block + 1, :]
-        level_line = gates[block : block + 1, :] - (line + before)
-        before = before + line[:, tokens - 1 : tokens]
-        level[:, block * tokens : (block + 1) * tokens] = level_line
-        spread = jnp.where(along <= across, jnp.broadcast_to(level_line, (tokens, tokens)), LOW)
-        tops = jnp.maximum(jnp.max(spread, axis=1, keepdims=True), peak)
-        peak = jnp.maximum(peak, jnp.max(level_line, axis=1, keepdims=True))
-        for j in range(CHUNKS):
-            top[j, block * part : (block + 1) * part, :] = tops[j * part : (j + 1) * part, :]
-    for slot in range(devices):
-        told = info.at[peer(slot)] if slot else info.at[me]
-        line = jnp.where(told[16:17, :].astype(jnp.int32) == me, told[18:19, :], 0.0) + jnp.where(
-            told[17:18, :].astype(jnp.int32) == me, told[19:20, :], 0.0
-        )
-        spread = jnp.where(along == across, jnp.broadcast_to(line, (tokens, tokens)), 0.0)
-        column = jnp.sum(spread, axis=1, keepdims=True)
-        place = SLOT_ORDER.index(slot) * part
-        for j in range(CHUNKS):
-            slot_weight[j, place : place + part, :] = column[j * part : (j + 1) * part, :]
-
-    arrive(key_all.at[tokens:, :], key_recv.at[0])
-    arrive(value_all.at[tokens:, :], value_recv.at[0])
-    loads[0].wait()
-    loads[1].wait()
-    place_in = lax.broadcasted_iota(jnp.int32, (devices * part, 1), 0)
-    place_in = lax.shift_right_logical(place_in, part.bit_length() - 1) * (tokens - part) + place_in
-    place_key = lax.broadcasted_iota(jnp.int32, (1, devices * tokens), 1)
-    for j in range(CHUNKS):
-        arrive(query_all.at[j, part:, :], query_recv.at[j])
-        loads[6 + j].wait()
-        scores = lax.dot_general(
-            query_all[j],
-            key_all[...],
-            (((1,), (1,)), ((), ())),
-            preferred_element_type=jnp.float32,
-        )
-        decay = jnp.exp(jnp.minimum(level[...] - top[j], 0.0))
-        coef = jnp.where(place_key <= place_in + j * part, decay * scores, 0.0) * (
-            1.0 / math.sqrt(head_dim)
-        )
-        denom_sum = jnp.sum(coef, axis=1, keepdims=True)
-        numer_sum = jnp.dot(
-            coef.astype(jnp.bfloat16), value_all[...], preferred_element_type=jnp.float32
-        )
-        mixed[j] = (numer_sum / jnp.maximum(jnp.abs(denom_sum), 1.0)).astype(jnp.bfloat16)
-        for flip in FLIPS:
+        lines = local_sum[block * heads : (block + 1) * heads, :]
+        level_lines = info[block, 0:8, :] - (lines + before)
+        before = before + lines[:, tokens - 1 : tokens]
+        level[block] = level_lines
+        peak_before[block] = jnp.broadcast_to(peak, (heads, tokens))
+        peak = jnp.maximum(peak, jnp.max(level_lines, axis=1, keepdims=True))
+    for group, first_chip in ((0, query_chip), (1, chip_x)):
+        for i in range(2):
+            head = (row if group else 1 - row) * (heads // 2) + 2 * core + i
+            for slot in range(4):
+                block = 2 * (chip if slot < 2 else first_chip) + slot % 2
+                line = level[block, pl.ds(head, 1), :]
+                if slot < 2:
+                    key_level[2 * group + i, :, slot * tokens : (slot + 1) * tokens] = line
+                spread = jnp.where(along <= across, jnp.broadcast_to(line, (tokens, tokens)), LOW)
+                tops = jnp.maximum(
+                    jnp.max(spread, axis=1, keepdims=True),
+                    peak_before[block, pl.ds(head, 1), :][:, 0:1],
+                )
+                for j in range(CHUNKS):
+                    top[j, slot * part : (slot + 1) * part, 2 * group + i : 2 * group + i + 1] = (
+                        tops[j * part : (j + 1) * part, :]
+                    )
+            if group == 0:
+                for slot in (2, 3):
+                    key_level[i, :, slot * tokens : (slot + 1) * tokens] = level[
+                        2 * key_chip + slot % 2, pl.ds(head, 1), :
+                    ]
+
+    query_row = lax.broadcasted_iota(jnp.int32, (4 * part, 1), 0)
+    row_block = lax.shift_right_logical(query_row, part.bit_length() - 1)
+    foreign_row = row_block >= 2
+    row_place = (
+        jnp.where(foreign_row, row_block - 2, row_block) * (tokens - part)
+        + query_row
+        - jnp.where(foreign_row, 2 * part, 0)
+    )
+    lane = lax.broadcasted_iota(jnp.int32, (2 * part, tokens), 1)
+    key_lane = lax.broadcasted_iota(jnp.int32, (1, 4 * tokens), 1)
+    wide_place = jnp.where(
+        key_lane < 2 * tokens,
+        chip * (2 * tokens) + key_lane,
+        key_chip * (2 * tokens) + key_lane - 2 * tokens,
+    )
+
+    def attend(j, group, query, key, value, key_place, foreign_chip, reply):
+        place = row_place + j * part + jnp.where(foreign_row, foreign_chip, chip) * (2 * tokens)
+        causal = key_place <= place
+        keys = key.shape[0]
+        extra = jnp.zeros((2 * part, tokens), jnp.float32)
+        for i in range(2):
+            number = 2 * group + i
+            view = slice(i * head_dim, (i + 1) * head_dim)
+            scores = lax.dot_general(
+                query[j, :, view],
+                key[:, view],
+                (((1,), (1,)), ((), ())),
+                preferred_element_type=jnp.float32,
+            )
+            decay = jnp.exp(
+                jnp.minimum(key_level[number, :, 0:keys] - top[j, :, number : number + 1], 0.0)
+            )
+            coef = jnp.where(causal, decay * scores, 0.0) * (1.0 / math.sqrt(head_dim))
+            denom_sum = jnp.sum(coef, axis=1, keepdims=True)
+            numer_sum = jnp.dot(
+                coef.astype(jnp.bfloat16), value[:, view], preferred_element_type=jnp.float32
+            )
+            for slot in range(2):
+                keep[j, group, i, :, slot * head_dim : (slot + 1) * head_dim] = numer_sum[
+                    slot * part : (slot + 1) * part, :
+                ]
+            denom[j, :, number : number + 1] = denom_sum[: 2 * part, :]
+            reply[j, :, view] = numer_sum[2 * part :, :].astype(jnp.bfloat16)
+            rest = denom_sum[2 * part :, :]
+            for term in range(3):
+                piece = rest.astype(jnp.bfloat16).astype(jnp.float32)
+                rest = rest - piece
+                extra = jnp.where(lane == 3 * i + term, piece, extra)
+        reply[j, :, slice_width:] = extra.astype(jnp.bfloat16)
+
+    def attend_slim(j):
+        @pl.when(column == 0)
+        def receive():
+            arrive(query_slim.at[j, 2 * part :, :], slim_recv.at[j])
+
+        attend(
+            j,
+            1,
+            query_slim,
+            key_slim,
+            value_slim,
+            chip * (2 * tokens) + key_lane[:, : 2 * tokens],
+            chip_x,
+            reply_slim,
+        )
+
+        @pl.when(column == 0)
+        def answer():
             remote(
-                mixed.at[j, block_rows(peer(flip), part), :],
-                mixer_in.at[j, :, head_columns(me)],
+                reply_slim.at[j], from_near_slim.at[j], reply_send.at[0], reply_recv.at[0, j], 2
+            )
+
+    def attend_wide(j):
+        arrive(query_wide.at[j, 2 * part :, :], wide_recv.at[j])
+        attend(j, 0, query_wide, key_wide, value_wide, wide_place, query_chip, reply_wide)
+
+        @pl.when(row == 0)
+        def answer_far():
+            remote(
+                reply_wide.at[j], from_far_row.at[j], reply_send.at[1], reply_recv.at[1, j], 4
+            )
+
+        @pl.when(row == 1)
+        def answer_near():
+            remote(
+                reply_wide.at[j], from_near_wide.at[j], reply_send.at[1], reply_recv.at[2, j], 2
+            )
+
+    def add_reply(j, group, number, source):
+        arrive(source.at[j], reply_recv.at[number, j])
+        extra = source[j, :, slice_width:].astype(jnp.float32)
+        for i in range(2):
+            for slot in range(2):
+                view = slice(slot * head_dim, (slot + 1) * head_dim)
+                keep[j, group, i, :, view] += source[
+                    j, slot * part : (slot + 1) * part, i * head_dim : (i + 1) * head_dim
+                ].astype(jnp.float32)
+            number = 2 * group + i
+            denom[j, :, number : number + 1] += (
+                extra[:, 3 * i : 3 * i + 1]
+                + extra[:, 3 * i + 1 : 3 * i + 2]
+                + extra[:, 3 * i + 2 : 3 * i + 3]
+            )
+
+    def settle(j):
+        @pl.when(row == 1)
+        def add_row():
+            add_reply(j, 1, 1, from_far_row)
+            add_reply(j, 0, 2, from_near_wide)
+
+        @pl.when(column == 1)
+        def add_column():
+            add_reply(j, 1, 0, from_near_slim)
+
+        for group in range(2):
+            for i in range(2):
+                number = 2 * group + i
+                for owner in (core, 1 - core):
+                    divisor = denom[j, span_of(owner, part), :][:, number : number + 1]
+                    value = (
+                        keep[j, group, i, :, span_of(owner, head_dim)]
+                        / jnp.maximum(jnp.abs(divisor), 1.0)
+                    ).astype(jnp.bfloat16)
+                    if owner is core:
+                        first = bases[group] + core * slice_width + i * head_dim
+                        mixer_in[j, :, pl.ds(pl.multiple_of(first, head_dim), head_dim)] = value
+                    else:
+                        first = group * slice_width + i * head_dim
+                        mixed[j, :, first : first + head_dim] = value
+            remote(
+                mixed.at[j, :, pl.ds(group * slice_width, slice_width)],
+                mixer_in.at[j, :, head_columns(bases[group], core)],
                 mixed_send.at[0],
                 mixed_recv.at[j],
-                flip,
-            )
-        mixer_in[j, :, head_columns(me)] = mixed[j, block_rows(me, part), :]
+                1,
+            )
+
+    def weigh():
+        for slot in range(devices):
+            told = info.at[peer(slot)] if slot else info.at[me]
+            line = jnp.where(
+                told[16:17, :].astype(jnp.int32) == me, told[18:19, :], 0.0
+            ) + jnp.where(told[17:18, :].astype(jnp.int32) == me, told[19:20, :], 0.0)
+            spread = jnp.where(along == across, jnp.broadcast_to(line, (tokens, tokens)), 0.0)
+            weight_column = jnp.sum(spread, axis=1, keepdims=True)
+            place = SLOT_ORDER.index(slot) * part
+            for j in range(CHUNKS):
+                slot_weight[j, place : place + part, :] = weight_column[
+                    j * part : (j + 1) * part, :
+                ]
 
     def slot_rows(slot):
         return pl.ds(SLOT_ORDER.index(slot) * part, part)
@@ -345,9 +533,9 @@
 
     gathers = {}
 
-    def gather(j, number, source, target, flip, half=None):
+    def gather(j, number, source, target, flip, half=None, begin=remote):
         view = slice(None) if half is None else columns(half)
-        gathers[j, number] = remote(
+        gathers[j, number] = begin(
             rows.at[j, slot_rows(source), view],
             rows.at[j, slot_rows(target), view],
             gather_send.at[0],
@@ -356,14 +544,14 @@
         )
 
     def normalise(j):
-        arrive(mixer_in.at[j, :, head_dim:], mixed_recv.at[j])
+        arrive(mixed.at[j], mixed_recv.at[j])
         if j == 0:
-            loads[2].wait()
+            large_loads[0].wait()
         span = slice(j * part, (j + 1) * part)
         mixer_out = mixer_in[j].astype(jnp.float32)
         square = jnp.mean(mixer_out * mixer_out, axis=1, keepdims=True)
         value = (
-            residual[span, :].astype(jnp.float32)
+            updated[span, :].astype(jnp.float32)
             + mixer_out * lax.rsqrt(square + EPSILON) * mix_gain[...]
         ).astype(jnp.bfloat16)
         updated[span, :] = value
@@ -373,12 +561,53 @@
             jnp.bfloat16
         )
 
-    def send_own(j):
-        gather(j, 0, 0, 2, 2, 0)
-        gather(j, 1, 0, 4, 4, 1)
-        gather(j, 2, 0, 2, 2, 1)
-        gather(j, 3, 0, 4, 4, 0)
-        gather(j, 4, 0, 1, 1)
+    def send_own(j, begin=remote):
+        gather(j, 0, 0, 2, 2, 0, begin)
+        gather(j, 1, 0, 4, 4, 1, begin)
+        gather(j, 2, 0, 2, 2, 1, begin)
+        gather(j, 3, 0, 4, 4, 0, begin)
+        gather(j, 4, 0, 1, 1, None, begin)
+
+    def attend_first():
+        place = row_place[: 2 * part, :] + chip * (2 * tokens)
+        causal = key_lane[:, : 2 * tokens] + chip * (2 * tokens) <= place
+        for group, query, key, value in (
+            (0, query_wide, key_wide, value_wide),
+            (1, query_slim, key_slim, value_slim),
+        ):
+            for i in range(2):
+                number = 2 * group + i
+                view = slice(i * head_dim, (i + 1) * head_dim)
+                scores = lax.dot_general(
+                    query[0, : 2 * part, view],
+                    key[: 2 * tokens, view],
+                    (((1,), (1,)), ((), ())),
+                    preferred_element_type=jnp.float32,
+                )
+                decay = jnp.exp(
+                    jnp.minimum(
+                        key_level[number, :, : 2 * tokens]
+                        - top[0, : 2 * part, number : number + 1],
+                        0.0,
+                    )
+                )
+                coef = jnp.where(causal, decay * scores, 0.0) * (1.0 / math.sqrt(head_dim))
+                denom[0, :, number : number + 1] = jnp.sum(coef, axis=1, keepdims=True)
+                numer_sum = jnp.dot(
+                    coef.astype(jnp.bfloat16),
+                    value[: 2 * tokens, view],
+                    preferred_element_type=jnp.float32,
+                )
+                for slot in range(2):
+                    keep[0, group, i, :, slot * head_dim : (slot + 1) * head_dim] = numer_sum[
+                        slot * part : (slot + 1) * part, :
+                    ]
+
+    def open_first():
+        settle(0)
+        normalise(0)
+        for number in (0, 1, 2):
+            gathers[0, number].start()
 
     def relay(j):
         gathers[j, 0].wait_recv()
@@ -401,8 +630,8 @@
         for number in (4, 7, 8, 9):
             gathers[j, number].wait_recv()
         if j == 0:
-            loads[3].wait()
-            loads[4].wait()
+            large_loads[1].wait()
+            large_loads[2].wait()
         for weight, total in ((gate, gate_sum), (up, up_sum)):
             total[...] = lax.dot_general(
                 rows[j],
@@ -413,7 +642,7 @@
         gate_val = gate_sum[...]
         hidden[...] = (gate_val / (1.0 + jnp.exp(-gate_val)) * up_sum[...]).astype(jnp.bfloat16)
         if j == 0:
-            loads[5].wait()
+            large_loads[3].wait()
         for half in range(HALVES):
             terms = (
                 jnp.dot(hidden[...], down[:, columns(half)], preferred_element_type=jnp.float32)
@@ -481,10 +710,57 @@
         for half in range(HALVES):
             step(j, half)
 
-    normalise(0)
-    send_own(0)
+    arrive(key_wide, pair_recv.at[CHUNKS])
+    for load in block_loads:
+        load.wait()
+    for j in range(CHUNKS):
+        arrive(query_wide.at[j, : 2 * part, :], pair_recv.at[j])
+
+    @pl.when(row == 1)
+    def slim_early():
+        for j in range(CHUNKS):
+            attend_slim(j)
+
+    send_own(0, prepared)
+
+    @pl.when(chip == 0)
+    def open_early():
+        attend_first()
+        open_first()
+
+    weigh()
+    arrive(key_wide, far_sem.at[1])
+    attend_wide(0)
+    attend_wide(1)
+
+    @pl.when(row == 0)
+    def slim_first():
+        attend_slim(0)
+
+    attend_wide(2)
+
+    @pl.when(row == 0)
+    def slim_second():
+        attend_slim(1)
+
+    attend_wide(3)
+
+    @pl.when(row == 0)
+    def slim_late():
+        attend_slim(2)
+        attend_slim(3)
+
+    @pl.when(chip > 0)
+    def open_late():
+        open_first()
+
+    gathers[0, 3].start()
+    gathers[0, 4].start()
+    settle(1)
     normalise(1)
     send_own(1)
+    settle(2)
+    settle(3)
     normalise(2)
     normalise(3)
     relay(0)
@@ -500,25 +776,41 @@
     relay(3)
     relay_last(2)
     both_halves(first_hop, 1)
+    compute(2)
     both_halves(second_hop, 0)
-    compute(2)
     relay_last(3)
     both_halves(first_hop, 2)
+    compute(3)
     both_halves(second_hop, 1)
-    both_halves(finish, 0)
-    compute(3)
     both_halves(first_hop, 3)
     both_halves(second_hop, 2)
+    both_halves(finish, 0)
     both_halves(finish, 1)
     both_halves(second_hop, 3)
     both_halves(finish, 2)
     both_halves(finish, 3)
+    @pl.when(row == 0)
+    def sent_keys():
+        arrive(rows.at[0], far_sem.at[0])
+
+    @pl.when(row == 1)
+    def sent_wide_queries():
+        arrive(key_wide, wide_send.at[0])
+
+    @pl.when(column == 1)
+    def sent_slim_queries():
+        arrive(key_slim, slim_send.at[0])
+
+    @pl.when(column == 0)
+    def sent_slim_replies():
+        arrive(reply_slim, reply_send.at[0])
+
+    arrive(key_slim, pair_send.at[1])
+    arrive(reply_wide, reply_send.at[1])
     for whole, flag in (
-        (info.at[1:], info_send),
-        (key_all.at[tokens:, :], key_send),
-        (value_all.at[tokens:, :], value_send),
-        (query_all.at[:, part:, :], query_send),
-        (mixed.at[:, part:, :], mixed_send),
+        (info.at[1:], info_sem),
+        (key_wide, pair_send),
+        (mixed, mixed_send),
         (rows.at[:, part:, :], gather_send),
         (core_out, core_send),
         (hop_out, hop_send),
@@ -558,16 +850,23 @@
             space(1, model_width, kind=jnp.float32),
             space(1, model_width, kind=jnp.float32),
             space(devices, 24, tokens, kind=jnp.float32),
-            space(2 * devices, tokens, kind=jnp.float32),
-            space(1, devices * tokens, kind=jnp.float32),
+            space(devices, devices, tokens, kind=jnp.float32),
+            space(devices, devices, tokens, kind=jnp.float32),
+            space(4, 1, 4 * tokens, kind=jnp.float32),
+            space(CHUNKS, 4 * part, 4, kind=jnp.float32),
             space(CHUNKS, batch, 1, kind=jnp.float32),
-            space(CHUNKS, batch, 1, kind=jnp.float32),
-            space(CHUNKS, batch, head_dim),
-            space(devices * tokens, head_dim),
-            space(devices * tokens, head_dim),
-            space(CHUNKS, batch, head_dim),
+            space(CHUNKS, 4 * part, 2 * head_dim),
+            space(CHUNKS, 4 * part, 2 * head_dim),
+            space(4 * tokens, 2 * head_dim),
+            space(4 * tokens, 2 * head_dim),
+            space(2 * tokens, 2 * head_dim),
+            space(2 * tokens, 2 * head_dim),
+        ]
+        + [space(CHUNKS, 2 * part, 2 * head_dim + tokens)] * 5
+        + [
+            space(CHUNKS, 2 * part, 4, kind=jnp.float32),
+            space(CHUNKS, part, 4 * head_dim),
             space(CHUNKS, part, model_width),
-            space(tokens, model_width),
             space(tokens, model_width),
             space(CHUNKS, batch, model_width),
             space(*gate_weight.shape),
@@ -584,12 +883,15 @@
             space(CHUNKS, HALVES, 2, part, width, kind=jnp.float32),
             space(CHUNKS, HALVES, part, width),
             space(CHUNKS, HALVES, part, width),
-            pltpu.SemaphoreType.DMA((12 + CHUNKS,)),
+            pltpu.SemaphoreType.DMA((14 + 2 * CHUNKS,)),
+            pltpu.SemaphoreType.DMA((2,)),
+            pltpu.SemaphoreType.DMA((2,)),
+            pltpu.SemaphoreType.DMA((CHUNKS + 1,)),
+            pltpu.SemaphoreType.DMA((2,)),
         ]
-        + flags(1)
-        + flags(1)
-        + flags(1)
         + flags(CHUNKS)
+        + flags(CHUNKS)
+        + [pltpu.SemaphoreType.DMA((2,)), pltpu.SemaphoreType.DMA((3, CHUNKS))]
         + flags(CHUNKS)
         + flags(CHUNKS, 10)
         + flags(CHUNKS, HALVES)

time: 123 us -> 113 us (0.919)
  Pallas kernels: 122 us -> 111 us
    pallas_call x1, Pallas kernels: 122 us -> 111 us  [fused_block(): pl.pallas_call(fused_kernel, out_shape=pltpu.VMEM((tokens, model_width),...]
where the time goes in v3:
time: 113 us; the launch traced here: 112 us
  Pallas kernels  111 us (98%)
    pallas_call x1, Pallas kernels, fused_block(): pl.pallas_call(fused_kernel, out_shape=pltpu.VMEM((tokens, model_width),...  111 us

profile of v3, /device:TPU:0, one launch (start us, length us, event | category | flops | bytes accessed | tf_op | source)
XLA Modules:
  0.0 111.6 jit_solution(657309412713584587)
XLA Ops:
  0.0 110.6 %shard_map.127 = bf16[128,4096]{1,0:T(8,128)(2,1)S(1)} custom-call(bf16[128,4096]{1,0:T(8,128)(2,1)} %query_far.1, bf16[128,4096]{1,0:T(8,128)(2,1)} %key_far.1, bf16[128,4096]{1,0:T(8,128)(2,1)} %value_far.1, bf16[128,4096]{1,0:T(8,128)(2,1)} %residual_far.1, f32[8,128]{1,0:T(8,128)} %input_far.1, f32[8,128]{1,0:T(8,128)} %forget_far.1, s32[2,128]{1,0:T(2,128)} %bitcast.16, ...), custom_call_target="tpu_custom_call" | custom-call | tf_op jit(solution)/shard_map/pallas_call | solution.py:840
  110.6 1.0 copy.15

commit v4 on v3

--- a/solution.py
+++ b/solution.py
@@ -124,6 +124,8 @@
     from_near_wide,
     from_near_slim,
     denom,
+    denom_out,
+    denom_in,
     mixed,
     mixer_in,
     updated,
@@ -153,6 +155,8 @@
     slim_recv,
     reply_send,
     reply_recv,
+    denom_send,
+    denom_recv,
     mixed_send,
     mixed_recv,
     gather_send,
@@ -268,7 +272,7 @@
     info[me, 18:20, :] = weights[...]
     pl.semaphore_wait(barrier, devices - 1)
 
-    for flip in FLIPS:
+    for flip in (6, 4, 2, 1):
         remote(info.at[me], info.at[me], info_sem.at[0], info_sem.at[1], flip)
 
     @pl.when(row == 0)
@@ -332,7 +336,11 @@
     for load in large_loads:
         load.start()
 
-    arrive(info.at[1:], info_sem.at[1])
+    arrive(info.at[:4], info_sem.at[1])
+    for flip in (2, 4, 6):
+        told = info.at[peer(flip)]
+        remote(told, told, info_sem.at[2], info_sem.at[3], 1)
+    arrive(info.at[:3], info_sem.at[3])
     across = lax.broadcasted_iota(jnp.int32, (tokens, tokens), 0)
     along = lax.broadcasted_iota(jnp.int32, (tokens, tokens), 1)
     local_sum = jnp.dot(
@@ -381,7 +389,7 @@
         + query_row
         - jnp.where(foreign_row, 2 * part, 0)
     )
-    lane = lax.broadcasted_iota(jnp.int32, (2 * part, tokens), 1)
+    diagonal = across[: 2 * part, :] == along[: 2 * part, :]
     key_lane = lax.broadcasted_iota(jnp.int32, (1, 4 * tokens), 1)
     wide_place = jnp.where(
         key_lane < 2 * tokens,
@@ -393,7 +401,6 @@
         place = row_place + j * part + jnp.where(foreign_row, foreign_chip, chip) * (2 * tokens)
         causal = key_place <= place
         keys = key.shape[0]
-        extra = jnp.zeros((2 * part, tokens), jnp.float32)
         for i in range(2):
             number = 2 * group + i
             view = slice(i * head_dim, (i + 1) * head_dim)
@@ -417,12 +424,21 @@
                 ]
             denom[j, :, number : number + 1] = denom_sum[: 2 * part, :]
             reply[j, :, view] = numer_sum[2 * part :, :].astype(jnp.bfloat16)
-            rest = denom_sum[2 * part :, :]
-            for term in range(3):
-                piece = rest.astype(jnp.bfloat16).astype(jnp.float32)
-                rest = rest - piece
-                extra = jnp.where(lane == 3 * i + term, piece, extra)
-        reply[j, :, slice_width:] = extra.astype(jnp.bfloat16)
+            denom_out[group, j, i : i + 1, :] = jnp.sum(
+                jnp.where(diagonal, denom_sum[2 * part :, :], 0.0), axis=0, keepdims=True
+            )
+
+    def answer(j, group, number, reply, target, flip):
+        remote(
+            reply.at[j], target.at[j], reply_send.at[group], reply_recv.at[number, j], flip
+        )
+        remote(
+            denom_out.at[group, j],
+            denom_in.at[number, j],
+            denom_send.at[group],
+            denom_recv.at[number, j],
+            flip,
+        )
 
     def attend_slim(j):
         @pl.when(column == 0)
@@ -441,10 +457,8 @@
         )
 
         @pl.when(column == 0)
-        def answer():
-            remote(
-                reply_slim.at[j], from_near_slim.at[j], reply_send.at[0], reply_recv.at[0, j], 2
-            )
+        def answer_slim():
+            answer(j, 1, 0, reply_slim, from_near_slim, 2)
 
     def attend_wide(j):
         arrive(query_wide.at[j, 2 * part :, :], wide_recv.at[j])
@@ -452,30 +466,26 @@
 
         @pl.when(row == 0)
         def answer_far():
-            remote(
-                reply_wide.at[j], from_far_row.at[j], reply_send.at[1], reply_recv.at[1, j], 4
-            )
+            answer(j, 0, 1, reply_wide, from_far_row, 4)
 
         @pl.when(row == 1)
         def answer_near():
-            remote(
-                reply_wide.at[j], from_near_wide.at[j], reply_send.at[1], reply_recv.at[2, j], 2
-            )
+            answer(j, 0, 2, reply_wide, from_near_wide, 2)
 
     def add_reply(j, group, number, source):
         arrive(source.at[j], reply_recv.at[number, j])
-        extra = source[j, :, slice_width:].astype(jnp.float32)
+        arrive(denom_in.at[number, j], denom_recv.at[number, j])
         for i in range(2):
             for slot in range(2):
                 view = slice(slot * head_dim, (slot + 1) * head_dim)
                 keep[j, group, i, :, view] += source[
                     j, slot * part : (slot + 1) * part, i * head_dim : (i + 1) * head_dim
                 ].astype(jnp.float32)
-            number = 2 * group + i
-            denom[j, :, number : number + 1] += (
-                extra[:, 3 * i : 3 * i + 1]
-                + extra[:, 3 * i + 1 : 3 * i + 2]
-                + extra[:, 3 * i + 2 : 3 * i + 3]
+            place = 2 * group + i
+            denom[j, :, place : place + 1] += jnp.sum(
+                jnp.where(diagonal, denom_in[number, j, i : i + 1, :], 0.0),
+                axis=1,
+                keepdims=True,
             )
 
     def settle(j):
@@ -803,12 +813,15 @@
 
     @pl.when(column == 0)
     def sent_slim_replies():
-        arrive(reply_slim, reply_send.at[0])
-
+        arrive(reply_slim, reply_send.at[1])
+        arrive(denom_out.at[1], denom_send.at[1])
+
+    arrive(info.at[:3], info_sem.at[2])
     arrive(key_slim, pair_send.at[1])
-    arrive(reply_wide, reply_send.at[1])
+    arrive(reply_wide, reply_send.at[0])
+    arrive(denom_out.at[0], denom_send.at[0])
     for whole, flag in (
-        (info.at[1:], info_sem),
+        (info.at[:4], info_sem),
         (key_wide, pair_send),
         (mixed, mixed_send),
         (rows.at[:, part:, :], gather_send),
@@ -862,9 +875,11 @@
             space(2 * tokens, 2 * head_dim),
             space(2 * tokens, 2 * head_dim),
         ]
-        + [space(CHUNKS, 2 * part, 2 * head_dim + tokens)] * 5
+        + [space(CHUNKS, 2 * part, 2 * head_dim)] * 5
         + [
             space(CHUNKS, 2 * part, 4, kind=jnp.float32),
+            space(2, CHUNKS, 2, tokens, kind=jnp.float32),
+            space(3, CHUNKS, 2, tokens, kind=jnp.float32),
             space(CHUNKS, part, 4 * head_dim),
             space(CHUNKS, part, model_width),
             space(tokens, model_width),
@@ -884,14 +899,14 @@
             space(CHUNKS, HALVES, part, width),
             space(CHUNKS, HALVES, part, width),
             pltpu.SemaphoreType.DMA((14 + 2 * CHUNKS,)),
-            pltpu.SemaphoreType.DMA((2,)),
+            pltpu.SemaphoreType.DMA((4,)),
             pltpu.SemaphoreType.DMA((2,)),
             pltpu.SemaphoreType.DMA((CHUNKS + 1,)),
             pltpu.SemaphoreType.DMA((2,)),
         ]
         + flags(CHUNKS)
         + flags(CHUNKS)
-        + [pltpu.SemaphoreType.DMA((2,)), pltpu.SemaphoreType.DMA((3, CHUNKS))]
+        + [pltpu.SemaphoreType.DMA((2,)), pltpu.SemaphoreType.DMA((3, CHUNKS))] * 2
         + flags(CHUNKS)
         + flags(CHUNKS, 10)
         + flags(CHUNKS, HALVES)

time: 113 us -> 111 us (0.982); the launches traced: 112 us -> 111 us
  no operation moved by 1% of the time
where the time goes in v4:
time: 111 us
  Pallas kernels  110 us (99%)
    pallas_call x1, Pallas kernels, fused_block(): pl.pallas_call(fused_kernel, out_shape=pltpu.VMEM((tokens, model_width),...  110 us

profile of v4, /device:TPU:0, one launch (start us, length us, event | category | flops | bytes accessed | tf_op | source)
XLA Modules:
  0.0 110.8 jit_solution(9708362129210853751)
XLA Ops:
  0.0 109.8 %shard_map.127 = bf16[128,4096]{1,0:T(8,128)(2,1)S(1)} custom-call(bf16[128,4096]{1,0:T(8,128)(2,1)} %query_far.1, bf16[128,4096]{1,0:T(8,128)(2,1)} %key_far.1, bf16[128,4096]{1,0:T(8,128)(2,1)} %value_far.1, bf16[128,4096]{1,0:T(8,128)(2,1)} %residual_far.1, f32[8,128]{1,0:T(8,128)} %input_far.1, f32[8,128]{1,0:T(8,128)} %forget_far.1, s32[2,128]{1,0:T(2,128)} %bitcast.16, ...), custom_call_target="tpu_custom_call" | custom-call | tf_op jit(solution)/shard_map/pallas_call | solution.py:853
  109.8 1.0 copy.15

commit v5 on v4

--- a/solution.py
+++ b/solution.py
@@ -277,15 +277,19 @@
 
     @pl.when(row == 0)
     def send_keys():
-        for far, target in ((key_far, key_wide), (value_far, value_wide)):
-            for flip, base in ((2, wide_base), (4, slim_base), (3, wide_base), (5, slim_base)):
-                remote(
-                    far.at[:, head_columns(base, core_of(flip))],
-                    target.at[span_of(core, tokens, 2 * tokens), :],
-                    far_sem.at[0],
-                    far_sem.at[1],
-                    flip,
-                )
+        for i in range(2):
+            for far, target in ((key_far, key_wide), (value_far, value_wide)):
+                for flip, base in ((2, wide_base), (4, slim_base), (3, wide_base), (5, slim_base)):
+                    first = base + core_of(flip) * slice_width + i * head_dim
+                    remote(
+                        far.at[:, pl.ds(pl.multiple_of(first, head_dim), head_dim)],
+                        target.at[
+                            span_of(core, tokens, 2 * tokens), pl.ds(i * head_dim, head_dim)
+                        ],
+                        far_sem.at[0],
+                        far_sem.at[1 + i],
+                        flip,
+                    )
 
     @pl.when(column == 1)
     def send_slim_queries():
@@ -397,11 +401,11 @@
         key_chip * (2 * tokens) + key_lane - 2 * tokens,
     )
 
-    def attend(j, group, query, key, value, key_place, foreign_chip, reply):
+    def attend(j, group, query, key, value, key_place, foreign_chip, reply, parts):
         place = row_place + j * part + jnp.where(foreign_row, foreign_chip, chip) * (2 * tokens)
         causal = key_place <= place
         keys = key.shape[0]
-        for i in range(2):
+        for i in parts:
             number = 2 * group + i
             view = slice(i * head_dim, (i + 1) * head_dim)
             scores = lax.dot_general(
@@ -428,17 +432,22 @@
                 jnp.where(diagonal, denom_sum[2 * part :, :], 0.0), axis=0, keepdims=True
             )
 
-    def answer(j, group, number, reply, target, flip):
+    def answer(j, group, number, reply, target, flip, view, flag):
         remote(
-            reply.at[j], target.at[j], reply_send.at[group], reply_recv.at[number, j], flip
-        )
-        remote(
-            denom_out.at[group, j],
-            denom_in.at[number, j],
-            denom_send.at[group],
-            denom_recv.at[number, j],
+            reply.at[j, :, view],
+            target.at[j, :, view],
+            reply_send.at[group],
+            reply_recv.at[flag, j],
             flip,
         )
+        if flag == number:
+            remote(
+                denom_out.at[group, j],
+                denom_in.at[number, j],
+                denom_send.at[group],
+                denom_recv.at[number, j],
+                flip,
+            )
 
     def attend_slim(j):
         @pl.when(column == 0)
@@ -454,26 +463,33 @@
             chip * (2 * tokens) + key_lane[:, : 2 * tokens],
             chip_x,
             reply_slim,
+            (0, 1),
         )
 
         @pl.when(column == 0)
         def answer_slim():
-            answer(j, 1, 0, reply_slim, from_near_slim, 2)
-
-    def attend_wide(j):
-        arrive(query_wide.at[j, 2 * part :, :], wide_recv.at[j])
-        attend(j, 0, query_wide, key_wide, value_wide, wide_place, query_chip, reply_wide)
+            answer(j, 1, 0, reply_slim, from_near_slim, 2, pl.ds(0, slice_width), 0)
+
+    def attend_wide(j, i):
+        if i == 0:
+            arrive(query_wide.at[j, 2 * part :, :], wide_recv.at[j])
+        attend(j, 0, query_wide, key_wide, value_wide, wide_place, query_chip, reply_wide, (i,))
+        view = pl.ds(i * head_dim, head_dim)
 
         @pl.when(row == 0)
         def answer_far():
-            answer(j, 0, 1, reply_wide, from_far_row, 4)
+            answer(j, 0, 1, reply_wide, from_far_row, 4, view, 3 - 2 * i)
 
         @pl.when(row == 1)
         def answer_near():
-            answer(j, 0, 2, reply_wide, from_near_wide, 2)
+            answer(j, 0, 2, reply_wide, from_near_wide, 2, view, 4 - 2 * i)
 
     def add_reply(j, group, number, source):
-        arrive(source.at[j], reply_recv.at[number, j])
+        if number == 0:
+            arrive(source.at[j], reply_recv.at[number, j])
+        else:
+            arrive(source.at[j, :, :head_dim], reply_recv.at[number + 2, j])
+            arrive(source.at[j, :, head_dim:], reply_recv.at[number, j])
         arrive(denom_in.at[number, j], denom_recv.at[number, j])
         for i in range(2):
             for slot in range(2):
@@ -739,21 +755,26 @@
         open_first()
 
     weigh()
-    arrive(key_wide, far_sem.at[1])
-    attend_wide(0)
-    attend_wide(1)
+    arrive(key_slim, far_sem.at[1])
+    for j in range(CHUNKS // 2):
+        attend_wide(j, 0)
+    arrive(key_slim, far_sem.at[2])
+    attend_wide(0, 1)
+    attend_wide(1, 1)
 
     @pl.when(row == 0)
     def slim_first():
         attend_slim(0)
 
-    attend_wide(2)
+    attend_wide(2, 0)
+    attend_wide(2, 1)
 
     @pl.when(row == 0)
     def slim_second():
         attend_slim(1)
 
-    attend_wide(3)
+    attend_wide(3, 0)
+    attend_wide(3, 1)
 
     @pl.when(row == 0)
     def slim_late():
@@ -902,11 +923,12 @@
             pltpu.SemaphoreType.DMA((4,)),
             pltpu.SemaphoreType.DMA((2,)),
             pltpu.SemaphoreType.DMA((CHUNKS + 1,)),
-            pltpu.SemaphoreType.DMA((2,)),
+            pltpu.SemaphoreType.DMA((3,)),
         ]
         + flags(CHUNKS)
         + flags(CHUNKS)
-        + [pltpu.SemaphoreType.DMA((2,)), pltpu.SemaphoreType.DMA((3, CHUNKS))] * 2
+        + [pltpu.SemaphoreType.DMA((2,)), pltpu.SemaphoreType.DMA((5, CHUNKS))]
+        + [pltpu.SemaphoreType.DMA((2,)), pltpu.SemaphoreType.DMA((3, CHUNKS))]
         + flags(CHUNKS)
         + flags(CHUNKS, 10)
         + flags(CHUNKS, HALVES)

time: 111 us -> 111 us (level)
  no operation moved by 1% of the time
where the time goes in v5:
time: 111 us
  Pallas kernels  110 us (99%)
    pallas_call x1, Pallas kernels, fused_block(): pl.pallas_call(fused_kernel, out_shape=pltpu.VMEM((tokens, model_width),...  110 us

profile of v5, /device:TPU:0, one launch (start us, length us, event | category | flops | bytes accessed | tf_op | source)
XLA Modules:
  0.0 110.9 jit_solution(13761473697287764027)
XLA Ops:
  0.0 109.9 %shard_map.127 = bf16[128,4096]{1,0:T(8,128)(2,1)S(1)} custom-call(bf16[128,4096]{1,0:T(8,128)(2,1)} %query_far.1, bf16[128,4096]{1,0:T(8,128)(2,1)} %key_far.1, bf16[128,4096]{1,0:T(8,128)(2,1)} %value_far.1, bf16[128,4096]{1,0:T(8,128)(2,1)} %residual_far.1, f32[8,128]{1,0:T(8,128)} %input_far.1, f32[8,128]{1,0:T(8,128)} %forget_far.1, s32[2,128]{1,0:T(2,128)} %bitcast.16, ...), custom_call_target="tpu_custom_call" | custom-call | tf_op jit(solution)/shard_map/pallas_call | solution.py:874
  109.9 1.0 copy.15
